TPU v7x, 32 devices: a whole 2x2x4 slice. The times are simulated.
32 devices in a mesh: ctx: 4 (over y, core), exp: 8 (over z, x).
Axes of the slice: x: 2, y: 2, z: 4, core: 2. Of those that a mesh axis runs over, the one named last changes fastest.
Arguments:
- queries: bfloat16 [512, 64, 576], P('ctx', 'exp'), may hold values from -1024 to 1024
- latents: bfloat16 [512, 576], P('ctx'), may hold values from -6.1 to 6.1
- block_starts: int32 [8], replicated, may hold values from 0 to 448, as said below
- w_uv: bfloat16 [64, 512, 128], P('exp'), may hold values from -0.25 to 0.25
- moe_tokens: bfloat16 [1024, 7168], P('exp'), may hold values from -6 to 6
- expert_ids: int32 [1024, 2], P('exp'), may hold values from 0 to 7, as said below
- gate_weights: float32 [1024, 2], P('exp'), may hold values from 0.2 to 1
- w_gate: bfloat16 [8, 7168, 512], P('exp', None, 'ctx'), may hold values from -0.0625 to 0.0625
- w_up: bfloat16 [8, 7168, 512], P('exp', None, 'ctx'), may hold values from -0.0625 to 0.0625
- w_down: bfloat16 [8, 512, 7168], P('exp', 'ctx'), may hold values from -0.25 to 0.25
Outputs:
- attended: bfloat16 [512, 64, 128], P('ctx', 'exp')
- moe_out: bfloat16 [1024, 7168], P('exp', 'ctx')
Inputs may be any that keep to these rules, and one draw needn't show every extreme that they name: Token t has position block_starts[t // 64] + t % 64; block_starts is a permutation of the multiples of 64 below 512. `expert_ids`: each row names 2 different experts. In the rows of one index of exp, one expert, the same for every index, is named by exactly 48 rows, no expert by more, and the other experts' counts differ by at most one.
All inputs are finite; a program needn't handle non-finite values.
Results may differ from a plain program's by a relative error of at most 0.018.
Values may be sent and summed in bfloat16 or wider, within the bound.
A program may use at most 128 MiB of HBM per device.

v0:
```python
import functools
import math

import jax
import jax.numpy as jnp
from jax import lax
from jax.experimental import pallas as pl
from jax.experimental.pallas import tpu as pltpu
from jax.sharding import PartitionSpec as P

score_scale = (0.1 * math.log(40.0) + 1.0) ** 2 / math.sqrt(192.0)
neg_fill = -1e30


def token_positions(block_starts, token_index, half_block):
    block_index = token_index // half_block
    matches = block_index[:, None] == jnp.arange(block_starts.shape[0], dtype=jnp.int32)[None, :]
    first_pos = jnp.sum(jnp.where(matches, block_starts[None, :], 0), axis=1)
    return first_pos + token_index % half_block


def slot_targets(expert_ids, expert_count, capacity):
    token_count, picks = expert_ids.shape
    flat_ids = expert_ids.reshape(token_count * picks)
    onehot = (flat_ids[:, None] == jnp.arange(expert_count, dtype=jnp.int32)[None, :]).astype(
        jnp.int32
    )
    earlier = jnp.cumsum(onehot, axis=0) - onehot
    slot_index = jnp.sum(earlier * onehot, axis=1)
    return flat_ids * capacity + slot_index


def attention(queries, latents, block_starts, w_uv):
    query_tokens, head_count, entry_width = queries.shape
    lat_width = w_uv.shape[1]
    half_block = query_tokens // 2
    row_total = query_tokens * head_count
    flat_queries = queries.reshape(row_total, entry_width)
    own_index = lax.axis_index("ctx") * query_tokens + jnp.arange(query_tokens, dtype=jnp.int32)
    own_positions = token_positions(block_starts, own_index, half_block)
    query_positions = jnp.repeat(own_positions, head_count)
    shard_piece = lax.all_gather(latents, "ctx", axis=0, tiled=True)
    key_positions = token_positions(
        block_starts, jnp.arange(shard_piece.shape[0], dtype=jnp.int32), half_block
    )
    top_score = jnp.full((row_total,), neg_fill, jnp.float32)
    scores = (
        lax.dot_general(
            flat_queries, shard_piece, (((1,), (1,)), ((), ())), preferred_element_type=jnp.float32
        )
        * score_scale
    )
    visible = key_positions[None, :] <= query_positions[:, None]
    masked = jnp.where(visible, scores, neg_fill)
    new_top = jnp.maximum(top_score, jnp.max(masked, axis=1))
    weights = jnp.where(visible, jnp.exp(masked - new_top[:, None]), 0.0)
    totals = jnp.sum(weights, axis=1)
    blended = jnp.dot(
        weights.astype(jnp.bfloat16), shard_piece[:, :lat_width], preferred_element_type=jnp.float32
    )
    top_score, totals, blended = (new_top, totals, blended)
    latent_out = (
        (blended / totals[:, None])
        .astype(jnp.bfloat16)
        .reshape(query_tokens, head_count, lat_width)
    )
    attended = jnp.einsum(
        "shl,hlv->shv", latent_out, w_uv, preferred_element_type=jnp.float32
    ).astype(jnp.bfloat16)
    return attended


def routed_plain(moe_tokens, expert_ids, gate_weights, w_gate, w_up, w_down):
    token_count, picks = expert_ids.shape
    model_width = moe_tokens.shape[1]
    expert_count = lax.axis_size("exp")
    capacity = 3 * token_count * picks // (2 * expert_count)
    targets = slot_targets(expert_ids, expert_count, capacity)
    source_row = jnp.arange(token_count * picks, dtype=jnp.int32) // picks
    filled = jnp.zeros((expert_count * capacity,), jnp.int32).at[targets].set(source_row + 1)
    occupied = filled > 0
    gate_matrix = w_gate[0]
    up_matrix = w_up[0]
    down_matrix = w_down[0]
    picked_rows = moe_tokens[jnp.where(occupied, filled - 1, 0)]
    outgoing = jnp.where(occupied[:, None], picked_rows, 0).reshape(
        expert_count, capacity, model_width
    )
    arrived = lax.all_to_all(outgoing, "exp", split_axis=0, concat_axis=0, tiled=True)
    senders, slot_count, width_in = arrived.shape
    flat_rows = arrived.reshape(senders * slot_count, width_in)
    gate_h = jnp.dot(flat_rows, gate_matrix, preferred_element_type=jnp.float32)
    up_h = jnp.dot(flat_rows, up_matrix, preferred_element_type=jnp.float32)
    hidden = (jax.nn.silu(gate_h) * up_h).astype(jnp.bfloat16)
    rounded = jnp.dot(hidden, down_matrix, preferred_element_type=jnp.float32).astype(jnp.bfloat16)
    rounded = lax.optimization_barrier(rounded.reshape(senders, slot_count, width_in))
    summed = lax.psum_scatter(
        rounded.astype(jnp.float32).astype(jnp.bfloat16), "ctx", scatter_dimension=2, tiled=True
    ).astype(jnp.float32)
    returned = lax.all_to_all(
        summed.astype(jnp.bfloat16), "exp", split_axis=0, concat_axis=0, tiled=True
    ).astype(summed.dtype)
    out_width = returned.shape[2]
    gathered = returned.reshape(expert_count * capacity, out_width)[targets].reshape(
        token_count, picks, out_width
    )
    weighted = jnp.sum(gathered * gate_weights[:, :, None], axis=1)
    return weighted.astype(jnp.bfloat16)


def flip_bits(index, bits):
    flipped = index
    for bit in range(bits.bit_length()):
        if (bits >> bit) % 2:
            flipped = flipped + (1 << bit) * (1 - 2 * ((index // (1 << bit)) % 2))
    return flipped


def plan(count, heads):
    half = count // 2
    near, far = list(range(1, half)), list(range(half, count))
    steps = [0]
    for at in range(half):
        steps += near[at : at + 1] + far[at : at + 1]
    lags = (("forward", 0), ("pass_on", 1), ("compute", 2), ("sum_cores", 3), ("sum_rows", 4))
    left = list(range(heads))
    order = []
    for at in range(count + 4):
        for stage, lag in lags:
            if 0 <= at - lag < count:
                order += [(stage, steps[at - lag])]
        if at == 1:
            order += [("latents", 0)]
        if at >= 2:
            share = min(len(left), -(-heads // (half + 1)))
            order += [("attend", left.pop(0)) for _ in range(share)]
    return order


def dot_first(left, right):
    return lax.dot_general(
        left, right, (((0,), (0,)), ((), ())), preferred_element_type=jnp.float32
    )


def dot_f32(left, right):
    return jnp.dot(left, right, preferred_element_type=jnp.float32)


def routed_kernel(
    count, outgoing, own_rows, combine, latents, starts, gate_hbm, up_hbm, down_hbm,
    queries_hbm, uv_hbm, out_ref, attended_ref,
    gate_w, up_w, down_w, query_t, uv_w, every_latent, value_t, seen, arrived, kept, core_send, core_recv, row_send, row_recv,
    back_send, returned, load_sem, lat_s, lat_r,
    out_s, out_r, side_s, side_r, near_s, near_r, relay_s, relay_r,
    core_s, core_r, row_s, row_r, back_s, back_r,
):
    me = lax.axis_index("exp")
    ctx = lax.axis_index("ctx")
    core = ctx % 2
    other_core = ctx + 1 - 2 * core
    other_row = (ctx + 2) % 4
    width = outgoing.shape[2]

    loads = [
        pltpu.make_async_copy(gate_hbm.at[0], gate_w, load_sem.at[0]),
        pltpu.make_async_copy(up_hbm.at[0], up_w, load_sem.at[1]),
        pltpu.make_async_copy(down_hbm.at[0], down_w, load_sem.at[2]),
        pltpu.make_async_copy(queries_hbm, query_t, load_sem.at[3]),
        pltpu.make_async_copy(uv_hbm, uv_w, load_sem.at[4]),
    ]
    for load in loads:
        load.start()

    barrier = pltpu.get_barrier_semaphore()
    for k in range(1, count):
        pl.semaphore_signal(
            barrier, inc=1, device_id={"exp": flip_bits(me, k), "ctx": ctx},
            device_id_type=pl.DeviceIdType.MESH,
        )
    for peer in (other_core, other_row):
        pl.semaphore_signal(
            barrier, inc=1, device_id={"exp": me, "ctx": peer},
            device_id_type=pl.DeviceIdType.MESH,
        )
    pl.semaphore_wait(barrier, count + 1)

    def remote(source, target, send, recv, exp, ctx_at):
        return pltpu.make_async_remote_copy(
            src_ref=source, dst_ref=target, send_sem=send, recv_sem=recv,
            device_id={"exp": exp, "ctx": ctx_at}, device_id_type=pl.DeviceIdType.MESH,
        )

    def dispatch(k):
        to = flip_bits(me, k)
        return remote(
            outgoing.at[to], arrived.at[ctx, me], out_s.at[k], out_r.at[k], to, ctx
        )

    def across(k):
        block = arrived.at[ctx, flip_bits(me, k)]
        return remote(block, block, side_s.at[k], side_r.at[k], me, other_row)

    def beside(k):
        block = arrived.at[ctx, flip_bits(me, k)]
        return remote(block, block, near_s.at[k], near_r.at[k], me, other_core)

    def relay(k):
        block = arrived.at[other_row, flip_bits(me, k)]
        return remote(block, block, relay_s.at[k], relay_r.at[k], me, other_core)

    def core_swap(k):
        return remote(
            core_send.at[k], core_recv.at[k], core_s.at[k], core_r.at[k], me, other_core
        )

    def row_swap(k):
        return remote(
            row_send.at[k], row_recv.at[k], row_s.at[k], row_r.at[k], me, other_row
        )

    def give_back(k):
        to = flip_bits(me, k)
        return remote(
            back_send.at[k], returned.at[me], back_s.at[k], back_r.at[k], to, ctx
        )

    def own_latents(step, peer):
        return remote(
            latents, every_latent.at[ctx], lat_s.at[step], lat_r.at[step], me, peer
        )

    row_block = every_latent.at[other_row]
    latents_beside = own_latents(0, other_core)
    latents_across = own_latents(1, other_row)
    latents_relay = remote(row_block, row_block, lat_s.at[2], lat_r.at[2], me, other_core)
    latents_across.start()
    latents_beside.start()
    schedule = plan(count, query_t.shape[0])
    partners = [at for stage, at in schedule if stage == "forward" and at]
    for k in partners:
        dispatch(k).start()
    every_latent[ctx] = latents[...]

    tokens = latents.shape[0]
    half_block = tokens // 2
    lat_width = uv_w.shape[1]

    def gather_latents(_):
        latents_across.wait_recv()
        latents_relay.start()
        key_at = lax.broadcasted_iota(jnp.int32, (4 * tokens, tokens), 0)
        own_at = lax.broadcasted_iota(jnp.int32, (4 * tokens, tokens), 1)
        key_block = key_at // half_block
        key_start = jnp.zeros_like(key_at)
        for block in range(8):
            key_start = jnp.where(key_block == block, starts[block], key_start)
        own_start = jnp.where(own_at < half_block, starts[2 * ctx], starts[2 * ctx + 1])
        key_position = key_start + key_at % half_block
        seen[...] = (key_position <= own_start + own_at % half_block).astype(jnp.float32)
        latents_beside.wait_recv()
        latents_relay.wait_recv()
        for block in range(4):
            value_t[:, pl.ds(block * tokens, tokens)] = every_latent[block, :, :lat_width].T

    def attend(head):
        keys = every_latent[...].reshape(4 * tokens, latents.shape[1])
        scores = dot_f32(keys, query_t[head]) * score_scale
        visible = seen[...] > 0.5
        masked = jnp.where(visible, scores, neg_fill)
        top = jnp.max(masked, axis=0, keepdims=True)
        weights = jnp.where(visible, jnp.exp(masked - top), 0.0)
        totals = jnp.sum(weights, axis=0, keepdims=True)
        blended = dot_f32(value_t[...], weights.astype(jnp.bfloat16))
        latent_out = (blended / totals).astype(jnp.bfloat16)
        attended_ref[head] = dot_first(latent_out, uv_w[head]).astype(jnp.bfloat16)

    def columns(at):
        return pl.ds(pl.multiple_of(at * width, 128), width)

    def experts(k):
        at = flip_bits(me, k)
        rows = outgoing.shape[1]
        gate_h = jnp.zeros((rows, gate_w.shape[1]), jnp.float32)
        up_h = jnp.zeros((rows, up_w.shape[1]), jnp.float32)
        for quarter in range(4):
            span = pl.ds(quarter * width, width)
            block = own_rows[:, span] if k == 0 else arrived[quarter, at]
            gate_h += dot_f32(block, gate_w[span, :])
            up_h += dot_f32(block, up_w[span, :])
        hidden = (gate_h / (1.0 + jnp.exp(-gate_h)) * up_h).astype(jnp.bfloat16)
        mate = 1 - core
        for side in range(2):
            core_send[k, side] = dot_f32(hidden, down_w[:, columns(mate + 2 * side)]).astype(
                jnp.bfloat16
            )
        core_swap(k).start()
        for side in range(2):
            kept[k, side] = dot_f32(hidden, down_w[:, columns(core + 2 * side)]).astype(
                jnp.bfloat16
            )

    def pair_sum(k, side):
        return kept[k, side].astype(jnp.float32) + core_recv[k, side].astype(jnp.float32)

    def forward(k):
        if k:
            dispatch(k).wait_recv()
            across(k).start()
            beside(k).start()

    def pass_on(k):
        if k:
            across(k).wait_recv()
            relay(k).start()

    def compute(k):
        if k:
            beside(k).wait_recv()
            relay(k).wait_recv()
        experts(k)

    def sum_cores(k):
        core_swap(k).wait_recv()
        row_send[k] = pair_sum(k, 1 - ctx // 2).astype(jnp.bfloat16)
        row_swap(k).start()

    def sum_rows(k):
        row_swap(k).wait_recv()
        total = pair_sum(k, ctx // 2) + row_recv[k].astype(jnp.float32)
        if k:
            back_send[k] = total.astype(jnp.bfloat16)
            give_back(k).start()
        else:
            returned[me] = total.astype(jnp.bfloat16)

    stages = {
        "forward": forward, "pass_on": pass_on, "compute": compute, "sum_cores": sum_cores,
        "sum_rows": sum_rows, "attend": attend, "latents": gather_latents,
    }
    waiting = list(loads)
    for stage, at in schedule:
        if stage == "compute":
            while waiting:
                waiting.pop(0).wait()
        stages[stage](at)

    for k in partners:
        give_back(k).wait_recv()
    back = returned[...].reshape(combine.shape[1], width)
    high = combine[...].astype(jnp.bfloat16)
    low = (combine[...] - high.astype(jnp.float32)).astype(jnp.bfloat16)
    out_ref[...] = (dot_f32(high, back) + dot_f32(low, back)).astype(jnp.bfloat16)
    for copy in (latents_across, latents_beside, latents_relay):
        copy.wait_send()
    for k in [0] + partners:
        core_swap(k).wait_send()
        row_swap(k).wait_send()
        if k:
            for copy in (dispatch, across, beside, relay, give_back):
                copy(k).wait_send()


def window_fused(
    queries, latents, block_starts, w_uv, moe_tokens, expert_ids, gate_weights, w_gate, w_up, w_down
):
    queries = jnp.transpose(queries, (1, 2, 0))
    heads, entry_width, query_tokens = queries.shape
    lat_width, value_width = w_uv.shape[1:]
    key_count = lax.axis_size("ctx") * query_tokens
    token_count, picks = expert_ids.shape
    model_width = moe_tokens.shape[1]
    hidden_width = w_gate.shape[2]
    count = lax.axis_size("exp")
    width = model_width // lax.axis_size("ctx")
    capacity = 3 * token_count * picks // (2 * count)
    targets = slot_targets(expert_ids, count, capacity).reshape(token_count, picks)
    slots = jnp.arange(count * capacity, dtype=jnp.int32)
    chosen = jnp.zeros((count * capacity, token_count), jnp.bool_)
    combine = jnp.zeros((token_count, count * capacity), jnp.float32)
    for pick in range(picks):
        chosen = chosen | (slots[:, None] == targets[None, :, pick])
        combine = combine + jnp.where(
            slots[None, :] == targets[:, pick : pick + 1], gate_weights[:, pick : pick + 1], 0.0
        )
    chosen = chosen.astype(jnp.bfloat16)
    quarter = lax.dynamic_slice_in_dim(moe_tokens, lax.axis_index("ctx") * width, width, 1)
    outgoing = jnp.dot(chosen, quarter, preferred_element_type=jnp.float32)
    outgoing = outgoing.astype(jnp.bfloat16).reshape(count, capacity, width)
    mine = lax.dynamic_slice_in_dim(chosen, lax.axis_index("exp") * capacity, capacity, 0)
    own_rows = jnp.dot(mine, moe_tokens, preferred_element_type=jnp.float32).astype(jnp.bfloat16)
    vmem = pl.BlockSpec(memory_space=pltpu.VMEM)
    hbm = pl.BlockSpec(memory_space=pl.ANY)
    block = (capacity, width)
    dtype = jnp.bfloat16
    routed, attended = pl.pallas_call(
        functools.partial(routed_kernel, count),
        out_shape=(
            jax.ShapeDtypeStruct((token_count, width), dtype),
            jax.ShapeDtypeStruct((heads, query_tokens, value_width), dtype),
        ),
        in_specs=[vmem] * 4 + [pl.BlockSpec(memory_space=pltpu.SMEM)] + [hbm] * 5,
        out_specs=(vmem, vmem),
        scratch_shapes=[
            pltpu.VMEM((model_width, hidden_width), dtype),
            pltpu.VMEM((model_width, hidden_width), dtype),
            pltpu.VMEM((hidden_width, model_width), dtype),
            pltpu.VMEM(queries.shape, dtype),
            pltpu.VMEM(w_uv.shape, dtype),
            pltpu.VMEM((4,) + latents.shape, dtype),
            pltpu.VMEM((lat_width, key_count), dtype),
            pltpu.VMEM((key_count, query_tokens), jnp.float32),
            pltpu.VMEM((4, count) + block, dtype),
            pltpu.VMEM((count, 2) + block, dtype),
            pltpu.VMEM((count, 2) + block, dtype),
            pltpu.VMEM((count, 2) + block, dtype),
            pltpu.VMEM((count,) + block, dtype),
            pltpu.VMEM((count,) + block, dtype),
            pltpu.VMEM((count,) + block, dtype),
            pltpu.VMEM((count,) + block, dtype),
            pltpu.SemaphoreType.DMA((5,)),
            pltpu.SemaphoreType.DMA((3,)),
            pltpu.SemaphoreType.DMA((3,)),
        ]
        + [pltpu.SemaphoreType.DMA((count,))] * 14,
        compiler_params=pltpu.CompilerParams(
            collective_id=0, has_side_effects=True, vmem_limit_bytes=56 * 1024 * 1024
        ),
    )(
        outgoing, own_rows, combine, latents, block_starts, w_gate, w_up, w_down, queries, w_uv
    )
    return jnp.transpose(attended, (1, 0, 2)), routed


def shards(
    queries, latents, block_starts, w_uv, moe_tokens, expert_ids, gate_weights, w_gate, w_up, w_down
):
    count = lax.axis_size("exp")
    ways = lax.axis_size("ctx")
    token_count, picks = expert_ids.shape
    capacity = 3 * token_count * picks // (2 * count)
    fits = ways == 4 and count & (count - 1) == 0 and count >= 4 and capacity % 16 == 0
    fits = fits and moe_tokens.shape[1] % (128 * ways) == 0 and block_starts.shape[0] == 8
    if fits:
        return window_fused(
            queries, latents, block_starts, w_uv, moe_tokens, expert_ids, gate_weights,
            w_gate, w_up, w_down,
        )
    attended = attention(queries, latents, block_starts, w_uv)
    return attended, routed_plain(moe_tokens, expert_ids, gate_weights, w_gate, w_up, w_down)


def solution(mesh):
    in_specs = (
        P("ctx", "exp", None),
        P("ctx", None),
        P(),
        P("exp", None, None),
        P("exp", None),
        P("exp", None),
        P("exp", None),
        P("exp", None, "ctx"),
        P("exp", None, "ctx"),
        P("exp", "ctx", None),
    )
    out_specs = (P("ctx", "exp", None), P("exp", "ctx"))
    return jax.shard_map(shards, mesh=mesh, in_specs=in_specs, out_specs=out_specs, check_vma=False)
```

profile of v0, /device:TPU:8, one launch (start us, length us, event | category | flops | bytes accessed | tf_op | source)
XLA Modules:
  0.0 96.0 jit_solution(13309426549728782252)
XLA Ops:
  0.6 0.0 copy-start
  0.7 0.8 slice_bitcast_fusion.1
  1.5 0.8 copy.26
  2.3 0.1 eq.86
  2.4 0.1 eq.82
  2.6 0.6 reduce-window.6
  3.1 0.2 slice_reduce_fusion
  3.4 0.1 fusion.4
  3.5 0.1 reduce_sum.12
  3.6 0.1 copy.28
  3.7 0.7 multiply_add_fusion
  4.5 1.7 %copy.29.latents = bf16[128,576]{1,0:T(8,128)(2,1)} copy(bf16[128,576]{0,1:T(8,128)(2,1)} %param.11) | data formatting | bytes 294912 | tf_op args[1]
  6.2 0.8 select_add_fusion.combine
  7.0 0.0 copy-done
  7.0 1.3 %convolution_convert_fusion.own_rows = bf16[48,7168]{1,0:T(8,128)(2,1)} fusion(bf16[128,7168]{1,0:T(8,128)(2,1)S(1)} %copy-done, pred[384,128]{1,0:T(8,128)(4,1)S(1)} %fusion.1, s32[]{:T(128)S(6)} %select_n.14), kind=kOutput, calls=%fused_computation | convolution fusion | flops 88424448 | bytes 2529284 | tf_op jit(solution)/shard_map/dot_general | solution.py:391
  8.3 1.6 %convolution_convert_fusion.1 = bf16[384,1792]{1,0:T(8,128)(2,1)} fusion(bf16[128,7168]{1,0:T(8,128)(2,1)S(1)} %copy-done, s32[]{:T(128)S(6)} %select_n.13, s32[128]{0:T(128)S(1)} %get-tuple-element.17, s32[128]{0:T(128)S(1)} %get-tuple-element.16), kind=kOutput, calls=%fused_computation.1 | convolution fusion | flops 176996352 | bytes 1836036 | tf_op jit(solution)/shard_map/dot_general | solution.py:388
  9.9 82.5 %shard_map.113 = (bf16[128,1792]{1,0:T(8,128)(2,1)}, bf16[8,128,128]{2,1,0:T(8,128)(2,1)}) custom-call(bf16[8,48,1792]{2,1,0:T(8,128)(2,1)} %bitcast.20, bf16[48,7168]{1,0:T(8,128)(2,1)} %convolution_convert_fusion.own_rows, f32[128,384]{1,0:T(8,128)} %select_add_fusion.combine, bf16[128,576]{1,0:T(8,128)(2,1)} %copy.29.latents, s32[8]{0:T(128)} %starts.1, ...), custom_call_target="tpu_custom_call" | custom-call | tf_op jit(solution)/shard_map/pallas_call | solution.py:396
  92.4 1.8 %copy.30 = bf16[128,8,128]{2,1,0:T(8,128)(2,1)} copy(bf16[128,8,128]{2,0,1:T(8,128)(2,1)} %bitcast.22) | data formatting | bytes 524288
  94.2 1.8 %copy.32 = bf16[128,1792]{1,0:T(8,128)(2,1)} copy(bf16[128,1792]{1,0:T(8,128)(2,1)} %get-tuple-element.21) | data formatting | bytes 917504
  (5 shorter events, 0.1 us)
Async XLA Ops:
  0.6 6.4 %copy-start = (bf16[128,7168]{1,0:T(8,128)(2,1)S(1)}, bf16[128,7168]{1,0:T(8,128)(2,1)}, u32[]{:S(2)}) copy-start(bf16[128,7168]{1,0:T(8,128)(2,1)} %param.14) | copy-start | bytes 5505028
where the time goes:
time: 96.3 us; the launch traced here: 96 us
  Pallas kernels  82.5 us (86%)
  local copies, waits for them, and re-layouts  7.68 us (8%)
  matrix products  2.87 us (3%)
  other arithmetic  2.28 us (2%)
    pallas_call x1, Pallas kernels, window_fused(): pl.pallas_call(functools.partial(routed_kernel, count), out_shape=(jax.Sh...  82.5 us
    unnamed x6, local copies, waits for them, and re-layouts  6.15 us

commit v1 on v0

v1 whole, which is shorter than its diff:
```python
import functools
import math

import jax
import jax.numpy as jnp
from jax import lax
from jax.experimental import pallas as pl
from jax.experimental.pallas import tpu as pltpu
from jax.sharding import PartitionSpec as P

score_scale = (0.1 * math.log(40.0) + 1.0) ** 2 / math.sqrt(192.0)
neg_fill = -1e30


def token_positions(block_starts, token_index, half_block):
    block_index = token_index // half_block
    matches = block_index[:, None] == jnp.arange(block_starts.shape[0], dtype=jnp.int32)[None, :]
    first_pos = jnp.sum(jnp.where(matches, block_starts[None, :], 0), axis=1)
    return first_pos + token_index % half_block


def slot_targets(expert_ids, expert_count, capacity):
    token_count, picks = expert_ids.shape
    flat_ids = expert_ids.reshape(token_count * picks)
    onehot = (flat_ids[:, None] == jnp.arange(expert_count, dtype=jnp.int32)[None, :]).astype(
        jnp.int32
    )
    earlier = jnp.cumsum(onehot, axis=0) - onehot
    slot_index = jnp.sum(earlier * onehot, axis=1)
    return flat_ids * capacity + slot_index


def attention(queries, latents, block_starts, w_uv):
    query_tokens, head_count, entry_width = queries.shape
    lat_width = w_uv.shape[1]
    half_block = query_tokens // 2
    row_total = query_tokens * head_count
    flat_queries = queries.reshape(row_total, entry_width)
    own_index = lax.axis_index("ctx") * query_tokens + jnp.arange(query_tokens, dtype=jnp.int32)
    own_positions = token_positions(block_starts, own_index, half_block)
    query_positions = jnp.repeat(own_positions, head_count)
    shard_piece = lax.all_gather(latents, "ctx", axis=0, tiled=True)
    key_positions = token_positions(
        block_starts, jnp.arange(shard_piece.shape[0], dtype=jnp.int32), half_block
    )
    top_score = jnp.full((row_total,), neg_fill, jnp.float32)
    scores = (
        lax.dot_general(
            flat_queries, shard_piece, (((1,), (1,)), ((), ())), preferred_element_type=jnp.float32
        )
        * score_scale
    )
    visible = key_positions[None, :] <= query_positions[:, None]
    masked = jnp.where(visible, scores, neg_fill)
    new_top = jnp.maximum(top_score, jnp.max(masked, axis=1))
    weights = jnp.where(visible, jnp.exp(masked - new_top[:, None]), 0.0)
    totals = jnp.sum(weights, axis=1)
    blended = jnp.dot(
        weights.astype(jnp.bfloat16), shard_piece[:, :lat_width], preferred_element_type=jnp.float32
    )
    top_score, totals, blended = (new_top, totals, blended)
    latent_out = (
        (blended / totals[:, None])
        .astype(jnp.bfloat16)
        .reshape(query_tokens, head_count, lat_width)
    )
    attended = jnp.einsum(
        "shl,hlv->shv", latent_out, w_uv, preferred_element_type=jnp.float32
    ).astype(jnp.bfloat16)
    return attended


def routed_plain(moe_tokens, expert_ids, gate_weights, w_gate, w_up, w_down):
    token_count, picks = expert_ids.shape
    model_width = moe_tokens.shape[1]
    expert_count = lax.axis_size("exp")
    capacity = 3 * token_count * picks // (2 * expert_count)
    targets = slot_targets(expert_ids, expert_count, capacity)
    source_row = jnp.arange(token_count * picks, dtype=jnp.int32) // picks
    filled = jnp.zeros((expert_count * capacity,), jnp.int32).at[targets].set(source_row + 1)
    occupied = filled > 0
    gate_matrix = w_gate[0]
    up_matrix = w_up[0]
    down_matrix = w_down[0]
    picked_rows = moe_tokens[jnp.where(occupied, filled - 1, 0)]
    outgoing = jnp.where(occupied[:, None], picked_rows, 0).reshape(
        expert_count, capacity, model_width
    )
    arrived = lax.all_to_all(outgoing, "exp", split_axis=0, concat_axis=0, tiled=True)
    senders, slot_count, width_in = arrived.shape
    flat_rows = arrived.reshape(senders * slot_count, width_in)
    gate_h = jnp.dot(flat_rows, gate_matrix, preferred_element_type=jnp.float32)
    up_h = jnp.dot(flat_rows, up_matrix, preferred_element_type=jnp.float32)
    hidden = (jax.nn.silu(gate_h) * up_h).astype(jnp.bfloat16)
    rounded = jnp.dot(hidden, down_matrix, preferred_element_type=jnp.float32).astype(jnp.bfloat16)
    rounded = lax.optimization_barrier(rounded.reshape(senders, slot_count, width_in))
    summed = lax.psum_scatter(
        rounded.astype(jnp.float32).astype(jnp.bfloat16), "ctx", scatter_dimension=2, tiled=True
    ).astype(jnp.float32)
    returned = lax.all_to_all(
        summed.astype(jnp.bfloat16), "exp", split_axis=0, concat_axis=0, tiled=True
    ).astype(summed.dtype)
    out_width = returned.shape[2]
    gathered = returned.reshape(expert_count * capacity, out_width)[targets].reshape(
        token_count, picks, out_width
    )
    weighted = jnp.sum(gathered * gate_weights[:, :, None], axis=1)
    return weighted.astype(jnp.bfloat16)


def flip_bits(index, bits):
    flipped = index
    for bit in range(bits.bit_length()):
        if (bits >> bit) % 2:
            flipped = flipped + (1 << bit) * (1 - 2 * ((index // (1 << bit)) % 2))
    return flipped


def plan(count, heads):
    half = count // 2
    near, far = list(range(1, half)), list(range(half, count))
    left = list(range(heads))
    order = [("compute", 0), ("latents", 0)]

    def attend(share):
        for _ in range(min(share, len(left))):
            order.append(("attend", left.pop(0)))

    attend(2)
    lags = (("forward", 0), ("pass_on", 1), ("compute", 1), ("down", 2))
    for at in range(len(far) + 2):
        if at < len(near):
            order.append(("forward", near[at]))
        if at < len(far):
            order.append(("forward", far[at]))
            order.append(("weights", at))
        if at < len(near):
            order.append(("compute", near[at]))
        if at == 1:
            attend(1)
        if 1 <= at <= len(far):
            order.append(("pass_on", far[at - 1]))
            attend(2)
            order.append(("compute", far[at - 1]))
        if at >= 2:
            order.append(("down", far[at - 2]))
            if at - 2 < len(near):
                order.append(("down", near[at - 2]))
    order.append(("down", 0))
    attend(len(left))
    return order


def dot_first(left, right):
    return lax.dot_general(
        left, right, (((0,), (0,)), ((), ())), preferred_element_type=jnp.float32
    )


def dot_f32(left, right):
    return jnp.dot(left, right, preferred_element_type=jnp.float32)


down_parts = 2


def window_kernel(
    count, capacity, wide, ids_hbm, gates_hbm, latents_hbm, tokens_hbm, starts_hbm, gate_hbm, up_hbm,
    down_hbm, queries_hbm, uv_hbm, out_ref, attended_ref,
    ids, gates, latents, tokens, starts, pair_w, down_w, query_t, uv_w, every_latent, keys, value_t, seen, place, gate_of,
    outgoing, arrived, hidden, back_send, returned,
    load_sem, lat_s, lat_r, out_s, out_r, side_s, side_r, near_s, near_r, relay_s, relay_r,
    hid_s, hid_r, wd_s, wd_r, back_s, back_r,
):
    me = lax.axis_index("exp")
    ctx = lax.axis_index("ctx")
    core = ctx % 2
    other_core = ctx + 1 - 2 * core
    other_row = (ctx + 2) % 4
    opposite = (other_core + 2) % 4
    peers = (other_core, other_row, opposite)
    width = outgoing.shape[3]
    token_count = tokens.shape[0]
    group = down_hbm.shape[1]
    part = group // down_parts
    fan = gate_hbm.shape[2]

    def columns(at):
        return pl.ds(pl.multiple_of(at * width, 128), width)

    inputs = [
        pltpu.make_async_copy(source, target, load_sem.at[5 + at])
        for at, (source, target) in enumerate(
            [(ids_hbm, ids), (tokens_hbm, tokens), (latents_hbm, latents), (gates_hbm, gates),
             (starts_hbm, starts)]
        )
    ]
    for load in inputs:
        load.start()
    loads = [
        pltpu.make_async_copy(gate_hbm.at[0], pair_w.at[:, pl.ds(0, fan)], load_sem.at[0]),
        pltpu.make_async_copy(up_hbm.at[0], pair_w.at[:, pl.ds(fan, fan)], load_sem.at[1]),
        pltpu.make_async_copy(queries_hbm, query_t, load_sem.at[3]),
        pltpu.make_async_copy(uv_hbm, uv_w, load_sem.at[4]),
        pltpu.make_async_copy(down_hbm.at[0, :, columns(ctx)], down_w.at[ctx], load_sem.at[2]),
    ]
    for load in loads:
        load.start()

    barrier = pltpu.get_barrier_semaphore()
    for k in range(1, count):
        pl.semaphore_signal(
            barrier, inc=1, device_id={"exp": flip_bits(me, k), "ctx": ctx},
            device_id_type=pl.DeviceIdType.MESH,
        )
    for peer in peers:
        pl.semaphore_signal(
            barrier, inc=1, device_id={"exp": me, "ctx": peer},
            device_id_type=pl.DeviceIdType.MESH,
        )

    def remote(source, target, send, recv, exp, ctx_at):
        return pltpu.make_async_remote_copy(
            src_ref=source, dst_ref=target, send_sem=send, recv_sem=recv,
            device_id={"exp": exp, "ctx": ctx_at}, device_id_type=pl.DeviceIdType.MESH,
        )

    def quarters(k):
        return (ctx, other_row) if k in wide else (ctx,)

    def dispatch(k):
        to = flip_bits(me, k)
        return [
            remote(
                outgoing.at[k, i], arrived.at[quarter, me], out_s.at[k, i], out_r.at[k, i], to, ctx
            )
            for i, quarter in enumerate(quarters(k))
        ]

    def across(k):
        block = arrived.at[ctx, flip_bits(me, k)]
        return remote(block, block, side_s.at[k], side_r.at[k], me, other_row)

    def beside(k):
        return [
            remote(
                arrived.at[quarter, flip_bits(me, k)], arrived.at[quarter, flip_bits(me, k)],
                near_s.at[k, i], near_r.at[k, i], me, other_core,
            )
            for i, quarter in enumerate(quarters(k))
        ]

    def relay(k):
        block = arrived.at[other_row, flip_bits(me, k)]
        return remote(block, block, relay_s.at[k], relay_r.at[k], me, other_core)

    def share_hidden(k):
        block = hidden.at[k, ctx]
        return [
            remote(block, block, hid_s.at[k, i], hid_r.at[k, i], me, peer)
            for i, peer in enumerate(peers)
        ]

    def share_down(i, piece):
        rows = pl.ds(piece * part, part)
        return remote(
            down_hbm.at[0, rows, columns(peers[i])], down_w.at[ctx, rows],
            wd_s.at[i, piece], wd_r.at[i, piece], me, peers[i],
        )

    def give_back(k):
        to = flip_bits(me, k)
        return remote(
            back_send.at[k], returned.at[me], back_s.at[k], back_r.at[k], to, ctx
        )

    def own_latents(step, peer):
        return remote(
            latents, every_latent.at[ctx], lat_s.at[step], lat_r.at[step], me, peer
        )

    row_block = every_latent.at[other_row]
    latents_beside = own_latents(0, other_core)
    latents_across = own_latents(1, other_row)
    latents_relay = remote(row_block, row_block, lat_s.at[2], lat_r.at[2], me, other_core)

    inputs[0].wait()
    inputs[3].wait()
    expert_at = lax.broadcasted_iota(jnp.int32, (count, token_count), 0)
    first, second = ids[0:1, :] == expert_at, ids[1:2, :] == expert_at
    member = first | second
    before = lax.broadcasted_iota(jnp.int32, (token_count, token_count), 0)
    after = lax.broadcasted_iota(jnp.int32, (token_count, token_count), 1)
    earlier = dot_f32(
        member.astype(jnp.float32).astype(jnp.bfloat16),
        (before < after).astype(jnp.float32).astype(jnp.bfloat16),
    )
    place[...] = jnp.where(member, earlier, -1.0)
    gate_of[...] = jnp.where(first, gates[0:1, :], 0.0) + jnp.where(second, gates[1:2, :], 0.0)
    slot_at = lax.broadcasted_iota(jnp.int32, (capacity, token_count), 0).astype(jnp.float32)

    def chosen(expert):
        return (place[pl.ds(expert, 1), :] == slot_at).astype(jnp.float32).astype(jnp.bfloat16)

    half = count // 2
    far, near = list(range(half, count)), list(range(1, half))

    def select(ks, i, column):
        picks = jnp.concatenate([chosen(flip_bits(me, k)) for k in ks], axis=0)
        rows = dot_f32(picks, tokens[:, columns(column)]).astype(jnp.bfloat16)
        for at, k in enumerate(ks):
            outgoing[k, i] = rows[at * capacity : (at + 1) * capacity]

    inputs[1].wait()
    select(far, 0, ctx)
    inputs[2].wait()
    pl.semaphore_wait(barrier, count + 2)
    latents_across.start()
    latents_beside.start()
    share_down(0, 0).start()
    for piece in range(1, down_parts):
        share_down(0, piece).start()
    for k in far:
        for copy in dispatch(k):
            copy.start()
    share_down(1, 0).start()
    share_down(2, 0).start()
    select(near, 0, ctx)
    if wide:
        select(list(wide), 1, other_row)
    for k in near:
        for copy in dispatch(k):
            copy.start()
    every_latent[ctx] = latents[...]
    mine = chosen(me)
    for quarter in range(4):
        span = pl.ds(quarter * width, width)
        arrived[quarter, me] = dot_f32(mine, tokens[:, span]).astype(jnp.bfloat16)

    span_tokens = latents.shape[1]
    half_block = span_tokens // 2
    lat_width = uv_w.shape[1]

    def gather_latents(_):
        latents_across.wait_recv()
        latents_relay.start()
        inputs[4].wait()
        key_at = lax.broadcasted_iota(jnp.int32, (4 * span_tokens, span_tokens), 0)
        own_at = lax.broadcasted_iota(jnp.int32, (4 * span_tokens, span_tokens), 1)
        key_block = key_at // half_block
        key_start = jnp.zeros_like(key_at)
        for block in range(8):
            key_start = jnp.where(key_block == block, starts[block], key_start)
        own_start = jnp.where(own_at < half_block, starts[2 * ctx], starts[2 * ctx + 1])
        key_position = key_start + key_at % half_block
        seen[...] = (key_position <= own_start + own_at % half_block).astype(jnp.float32)
        latents_beside.wait_recv()
        latents_relay.wait_recv()
        for block in range(4):
            span = pl.ds(block * span_tokens, span_tokens)
            value_t[:, span] = every_latent[block, :lat_width, :]
            keys[span, :] = every_latent[block].T
        for load in loads[2:4]:
            load.wait()

    def attend(head):
        scores = dot_f32(keys[...], query_t[head]) * score_scale
        visible = seen[...] > 0.5
        masked = jnp.where(visible, scores, neg_fill)
        top = jnp.max(masked, axis=0, keepdims=True)
        weights = jnp.where(visible, jnp.exp(masked - top), 0.0)
        totals = jnp.sum(weights, axis=0, keepdims=True)
        blended = dot_f32(value_t[...], weights.astype(jnp.bfloat16))
        latent_out = (blended / totals).astype(jnp.bfloat16)
        attended_ref[head] = dot_first(latent_out, uv_w[head]).astype(jnp.bfloat16)

    def forward(k):
        for copy in dispatch(k):
            copy.wait_recv()
        if k not in wide:
            across(k).start()
        for copy in beside(k):
            copy.start()

    def weights(at):
        piece = at + 1
        if piece < down_parts:
            share_down(1, piece).start()
            share_down(2, piece).start()

    def pass_on(k):
        if k not in wide:
            across(k).wait_recv()
            relay(k).start()

    def compute(k):
        if k:
            for copy in beside(k):
                copy.wait_recv()
            if k not in wide:
                relay(k).wait_recv()
        else:
            loads[0].wait()
            loads[1].wait()
        at = flip_bits(me, k)
        both = jnp.zeros((capacity, 2 * fan), jnp.float32)
        for quarter in range(4):
            both += dot_f32(arrived[quarter, at], pair_w[pl.ds(quarter * width, width), :])
        gate_h, up_h = both[:, :fan], both[:, fan:]
        hidden[k, ctx] = (gate_h / (1.0 + jnp.exp(-gate_h)) * up_h).astype(jnp.bfloat16)
        for copy in share_hidden(k):
            copy.start()

    waiting = [loads[4]]

    def down(k):
        while waiting:
            waiting.pop().wait()
            for i in range(3):
                for piece in range(down_parts):
                    share_down(i, piece).wait_recv()
        for copy in share_hidden(k):
            copy.wait_recv()
        total = dot_f32(hidden[k, 0], down_w[0])
        for block in range(1, 4):
            total += dot_f32(hidden[k, block], down_w[block])
        if k:
            back_send[k] = total.astype(jnp.bfloat16)
            give_back(k).start()
        else:
            returned[me] = total.astype(jnp.bfloat16)

    stages = {
        "forward": forward, "pass_on": pass_on, "compute": compute, "down": down,
        "attend": attend, "latents": gather_latents, "weights": weights,
    }
    for stage, at in plan(count, query_t.shape[0]):
        stages[stage](at)

    spread = jnp.concatenate(
        [
            jnp.where(place[e : e + 1, :] == slot_at, gate_of[e : e + 1, :], 0.0)
            for e in range(count)
        ],
        axis=0,
    )
    high = spread.astype(jnp.bfloat16)
    low = (spread - high.astype(jnp.float32)).astype(jnp.bfloat16)
    for k in range(1, count):
        give_back(k).wait_recv()
    back = returned[...].reshape(count * capacity, width)
    out_ref[...] = (dot_first(high, back) + dot_first(low, back)).astype(jnp.bfloat16)
    for copy in (latents_across, latents_beside, latents_relay):
        copy.wait_send()
    for i in range(3):
        for piece in range(down_parts):
            share_down(i, piece).wait_send()
    for k in range(count):
        copies = share_hidden(k)
        if k:
            copies += dispatch(k) + beside(k) + [give_back(k)]
            if k not in wide:
                copies += [across(k), relay(k)]
        for copy in copies:
            copy.wait_send()


def window_fused(
    queries, latents, block_starts, w_uv, moe_tokens, expert_ids, gate_weights, w_gate, w_up, w_down
):
    queries = jnp.transpose(queries, (1, 2, 0))
    heads, entry_width, query_tokens = queries.shape
    lat_width, value_width = w_uv.shape[1:]
    ways = lax.axis_size("ctx")
    key_count = ways * query_tokens
    token_count, picks = expert_ids.shape
    model_width = moe_tokens.shape[1]
    fan = w_gate.shape[2]
    count = lax.axis_size("exp")
    width = model_width // ways
    capacity = 3 * token_count * picks // (2 * count)
    wide = tuple(range(1, count // 2))
    vmem = pl.BlockSpec(memory_space=pltpu.VMEM)
    hbm = pl.BlockSpec(memory_space=pltpu.HBM)
    block = (capacity, width)
    dtype = jnp.bfloat16
    dma = pltpu.SemaphoreType.DMA
    routed, attended = pl.pallas_call(
        functools.partial(window_kernel, count, capacity, wide),
        out_shape=(
            jax.ShapeDtypeStruct((token_count, width), dtype),
            jax.ShapeDtypeStruct((heads, query_tokens, value_width), dtype),
        ),
        in_specs=[hbm] * 10,
        out_specs=(vmem, vmem),
        scratch_shapes=[
            pltpu.VMEM((picks, token_count), jnp.int32),
            pltpu.VMEM((picks, token_count), jnp.float32),
            pltpu.VMEM((entry_width, query_tokens), dtype),
            pltpu.VMEM((token_count, model_width), dtype),
            pltpu.SMEM(block_starts.shape, jnp.int32),
            pltpu.VMEM((model_width, 2 * fan), dtype),
            pltpu.VMEM((ways, fan, width), dtype),
            pltpu.VMEM(queries.shape, dtype),
            pltpu.VMEM(w_uv.shape, dtype),
            pltpu.VMEM((ways, entry_width, query_tokens), dtype),
            pltpu.VMEM((key_count, entry_width), dtype),
            pltpu.VMEM((lat_width, key_count), dtype),
            pltpu.VMEM((key_count, query_tokens), jnp.float32),
            pltpu.VMEM((count, token_count), jnp.float32),
            pltpu.VMEM((count, token_count), jnp.float32),
            pltpu.VMEM((count, 2) + block, dtype),
            pltpu.VMEM((ways, count) + block, dtype),
            pltpu.VMEM((count, ways, capacity, fan), dtype),
            pltpu.VMEM((count,) + block, dtype),
            pltpu.VMEM((count,) + block, dtype),
            dma((10,)), dma((3,)), dma((3,)),
            dma((count, 2)), dma((count, 2)),
            dma((count,)), dma((count,)),
            dma((count, 2)), dma((count, 2)),
            dma((count,)), dma((count,)),
            dma((count, 3)), dma((count, 3)),
            dma((3, down_parts)), dma((3, down_parts)),
            dma((count,)), dma((count,)),
        ],
        compiler_params=pltpu.CompilerParams(
            collective_id=0, has_side_effects=True, vmem_limit_bytes=40 * 1024 * 1024
        ),
    )(
        *[
            pltpu.with_memory_space_constraint(operand, pltpu.HBM)
            for operand in (
                expert_ids.T, gate_weights.T, latents.T, moe_tokens, block_starts,
                w_gate, w_up, w_down, queries, w_uv,
            )
        ]
    )
    return jnp.transpose(attended, (1, 0, 2)), routed


def shards(
    queries, latents, block_starts, w_uv, moe_tokens, expert_ids, gate_weights, w_gate, w_up, w_down
):
    count = lax.axis_size("exp")
    ways = lax.axis_size("ctx")
    token_count, picks = expert_ids.shape
    capacity = 3 * token_count * picks // (2 * count)
    fits = ways == 4 and count & (count - 1) == 0 and count >= 4 and capacity % 16 == 0
    fits = fits and moe_tokens.shape[1] % (128 * ways) == 0 and block_starts.shape[0] == 8
    fits = fits and picks == 2 and w_gate.shape[2] % 128 == 0
    if fits:
        return window_fused(
            queries, latents, block_starts, w_uv, moe_tokens, expert_ids, gate_weights,
            w_gate, w_up, w_down,
        )
    attended = attention(queries, latents, block_starts, w_uv)
    return attended, routed_plain(moe_tokens, expert_ids, gate_weights, w_gate, w_up, w_down)


def solution(mesh):
    in_specs = (
        P("ctx", "exp", None),
        P("ctx", None),
        P(),
        P("exp", None, None),
        P("exp", None),
        P("exp", None),
        P("exp", None),
        P("exp", None, "ctx"),
        P("exp", None, "ctx"),
        P("exp", "ctx", None),
    )
    out_specs = (P("ctx", "exp", None), P("exp", "ctx"))
    return jax.shard_map(shards, mesh=mesh, in_specs=in_specs, out_specs=out_specs, check_vma=False)
```

time: 96.3 us -> 81.8 us (0.85)
  the two profiles are of different devices: /device:TPU:8 before, /device:TPU:0 now
where the time goes in v1:
time: 81.8 us; the launch traced here: 81.6 us
  Pallas kernels  79.3 us (97%)
  local copies, waits for them, and re-layouts  1.64 us (2%)
    pallas_call x1, Pallas kernels, window_fused(): pl.pallas_call(functools.partial(window_kernel, count, capacity, wide), o...  79.3 us
    unnamed x2, local copies, waits for them, and re-layouts  1.64 us

profile of v1, /device:TPU:0, one launch (start us, length us, event | category | flops | bytes accessed | tf_op | source)
XLA Modules:
  0.0 81.6 jit_solution(14827627455744697299)
XLA Ops:
  0.6 79.3 %shard_map.113 = (bf16[128,1792]{1,0:T(8,128)(2,1)S(1)}, bf16[8,128,128]{2,1,0:T(8,128)(2,1)S(1)}) custom-call(s32[2,128]{1,0:T(2,128)} %bitcast.8, f32[2,128]{1,0:T(2,128)} %bitcast.9, bf16[576,128]{1,0:T(8,128)(2,1)} %bitcast.7, bf16[128,7168]{1,0:T(8,128)(2,1)} %tokens_hbm.1, s32[8]{0:T(128)} %starts_hbm.1, bf16[1,7168,128]{2,1,0:T(8,128)(2,1)} %gate_hbm.1, ...), custom_call_target="tpu_custom_call" | custom-call | tf_op jit(solution)/shard_map/pallas_call | solution.py:488
  79.9 0.9 %copy.12 = bf16[128,8,128]{2,1,0:T(8,128)(2,1)} copy(bf16[128,8,128]{2,0,1:T(8,128)(2,1)S(1)} %bitcast.5) | data formatting | bytes 524288
  80.8 0.8 copy.14

commit v2 on v1

--- a/solution.py
+++ b/solution.py
@@ -116,38 +116,28 @@
     return flipped
 
 
+down_parts = 1
+
+
 def plan(count, heads):
     half = count // 2
     near, far = list(range(1, half)), list(range(half, count))
-    left = list(range(heads))
-    order = [("compute", 0), ("latents", 0)]
-
-    def attend(share):
-        for _ in range(min(share, len(left))):
-            order.append(("attend", left.pop(0)))
-
-    attend(2)
-    lags = (("forward", 0), ("pass_on", 1), ("compute", 1), ("down", 2))
-    for at in range(len(far) + 2):
-        if at < len(near):
-            order.append(("forward", near[at]))
-        if at < len(far):
-            order.append(("forward", far[at]))
-            order.append(("weights", at))
-        if at < len(near):
-            order.append(("compute", near[at]))
-        if at == 1:
-            attend(1)
-        if 1 <= at <= len(far):
-            order.append(("pass_on", far[at - 1]))
-            attend(2)
-            order.append(("compute", far[at - 1]))
-        if at >= 2:
-            order.append(("down", far[at - 2]))
-            if at - 2 < len(near):
-                order.append(("down", near[at - 2]))
-    order.append(("down", 0))
-    attend(len(left))
+    order = [("compute", 0)]
+    order += [("forward", k) for k in near[:-1]]
+    order += [("compute", k) for k in near[:-1]]
+    order += [("forward", far[0]), ("forward", near[-1]), ("compute", near[-1])]
+    order += [("down", 0)] + [("down", k) for k in near[:-1]]
+    order += [("forward", far[1]), ("pass_on", far[0]), ("down", near[-1]), ("compute", far[0])]
+    order += [("forward", far[2])]
+    for at in range(1, len(far)):
+        order += [("pass_on", far[at]), ("down", far[at - 1]), ("compute", far[at])]
+        if at + 2 < len(far):
+            order += [("forward", far[at + 2])]
+        elif at + 2 == len(far):
+            order += [("latents", 0)]
+    order += [("gather", 0), ("down", far[-1])]
+    order += [("attend", 0), ("attend", 2), ("settle", 0)]
+    order += [("attend", head) for head in range(4, heads, 2)]
     return order
 
 
@@ -161,16 +151,13 @@
     return jnp.dot(left, right, preferred_element_type=jnp.float32)
 
 
-down_parts = 2
-
-
 def window_kernel(
-    count, capacity, wide, ids_hbm, gates_hbm, latents_hbm, tokens_hbm, starts_hbm, gate_hbm, up_hbm,
+    count, capacity, base, wide, ids_hbm, gates_hbm, latents_hbm, tokens_hbm, starts_hbm, gate_hbm, up_hbm,
     down_hbm, queries_hbm, uv_hbm, out_ref, attended_ref,
     ids, gates, latents, tokens, starts, pair_w, down_w, query_t, uv_w, every_latent, keys, value_t, seen, place, gate_of,
-    outgoing, arrived, hidden, back_send, returned,
+    outgoing, far_rows, arrived, hidden, back_send, collected, settled, returned,
     load_sem, lat_s, lat_r, out_s, out_r, side_s, side_r, near_s, near_r, relay_s, relay_r,
-    hid_s, hid_r, wd_s, wd_r, back_s, back_r,
+    hid_s, hid_r, wd_s, wd_r, back_s, back_r, fan_s, fan_r, collect_s, collect_r, settle_s, settle_r,
 ):
     me = lax.axis_index("exp")
     ctx = lax.axis_index("ctx")
@@ -225,17 +212,44 @@
             device_id={"exp": exp, "ctx": ctx_at}, device_id_type=pl.DeviceIdType.MESH,
         )
 
+    half = count // 2
+    rest = capacity - base
+    far, near = list(range(half, count)), list(range(1, half))
+
+    def far_start(k):
+        return (k - half) * base + (rest if k > half else 0)
+
+    def rows_of(k):
+        return base if k > half else capacity
+
+    def slots(k):
+        if k < half:
+            return pl.ds(k * capacity, capacity)
+        return pl.ds(half * capacity + (k - half) * base, base)
+
+    extra_slots = pl.ds(half * (capacity + base), rest)
+    low_rows, high_rows = pl.ds(0, base), pl.ds(base, rest)
+
     def quarters(k):
         return (ctx, other_row) if k in wide else (ctx,)
 
     def dispatch(k):
         to = flip_bits(me, k)
+        if k >= half:
+            rows = rows_of(k)
+            source = far_rows.at[pl.ds(far_start(k), rows)]
+            target = arrived.at[ctx, me, pl.ds(0, rows)]
+            return [remote(source, target, out_s.at[k, 0], out_r.at[k, 0], to, ctx)]
         return [
             remote(
                 outgoing.at[k, i], arrived.at[quarter, me], out_s.at[k, i], out_r.at[k, i], to, ctx
             )
             for i, quarter in enumerate(quarters(k))
         ]
+
+    def fan_out(k):
+        block = arrived.at[ctx, flip_bits(me, half), high_rows]
+        return remote(block, block, fan_s.at[k], fan_r.at[k], flip_bits(me, k), ctx)
 
     def across(k):
         block = arrived.at[ctx, flip_bits(me, k)]
@@ -270,8 +284,19 @@
 
     def give_back(k):
         to = flip_bits(me, k)
+        source = back_send.at[k, low_rows] if k >= half else back_send.at[k]
+        return remote(source, returned.at[slots(k)], back_s.at[k], back_r.at[k], to, ctx)
+
+    def collect(k):
         return remote(
-            back_send.at[k], returned.at[me], back_s.at[k], back_r.at[k], to, ctx
+            back_send.at[k + half, high_rows], collected.at[k], collect_s.at[k], collect_r.at[k],
+            flip_bits(me, k), ctx,
+        )
+
+    def settle_extra():
+        return remote(
+            settled, returned.at[extra_slots], settle_s.at[0], settle_r.at[0],
+            flip_bits(me, half), ctx,
         )
 
     def own_latents(step, peer):
@@ -299,40 +324,47 @@
     gate_of[...] = jnp.where(first, gates[0:1, :], 0.0) + jnp.where(second, gates[1:2, :], 0.0)
     slot_at = lax.broadcasted_iota(jnp.int32, (capacity, token_count), 0).astype(jnp.float32)
 
-    def chosen(expert):
-        return (place[pl.ds(expert, 1), :] == slot_at).astype(jnp.float32).astype(jnp.bfloat16)
-
-    half = count // 2
-    far, near = list(range(half, count)), list(range(1, half))
+    def row_of(ref, k):
+        return ref[pl.ds(flip_bits(me, k), 1), :]
+
+    def one_hot(k, first_slot, last_slot):
+        return (row_of(place, k) == slot_at[first_slot:last_slot]).astype(jnp.float32)
+
+    def take(picks, column):
+        rows = dot_f32(picks.astype(jnp.bfloat16), tokens[:, columns(column)])
+        return rows.astype(jnp.bfloat16)
 
     def select(ks, i, column):
-        picks = jnp.concatenate([chosen(flip_bits(me, k)) for k in ks], axis=0)
-        rows = dot_f32(picks, tokens[:, columns(column)]).astype(jnp.bfloat16)
+        rows = take(jnp.concatenate([one_hot(k, 0, capacity) for k in ks], axis=0), column)
         for at, k in enumerate(ks):
             outgoing[k, i] = rows[at * capacity : (at + 1) * capacity]
 
+    def select_far():
+        picks = [one_hot(k, 0, base) for k in far]
+        extra = one_hot(half, base, capacity)
+        for k in far[1:]:
+            extra += one_hot(k, base, capacity)
+        far_rows[...] = take(jnp.concatenate(picks[:1] + [extra] + picks[1:], axis=0), ctx)
+
     inputs[1].wait()
-    select(far, 0, ctx)
+    select(near, 0, ctx)
+    if wide:
+        select(list(wide), 1, other_row)
     inputs[2].wait()
     pl.semaphore_wait(barrier, count + 2)
-    latents_across.start()
+    for k in near:
+        for copy in dispatch(k):
+            copy.start()
+    for i in (1, 2, 0):
+        for piece in range(down_parts):
+            share_down(i, piece).start()
     latents_beside.start()
-    share_down(0, 0).start()
-    for piece in range(1, down_parts):
-        share_down(0, piece).start()
+    select_far()
     for k in far:
         for copy in dispatch(k):
             copy.start()
-    share_down(1, 0).start()
-    share_down(2, 0).start()
-    select(near, 0, ctx)
-    if wide:
-        select(list(wide), 1, other_row)
-    for k in near:
-        for copy in dispatch(k):
-            copy.start()
     every_latent[ctx] = latents[...]
-    mine = chosen(me)
+    mine = one_hot(0, 0, capacity).astype(jnp.bfloat16)
     for quarter in range(4):
         span = pl.ds(quarter * width, width)
         arrived[quarter, me] = dot_f32(mine, tokens[:, span]).astype(jnp.bfloat16)
@@ -340,6 +372,9 @@
     span_tokens = latents.shape[1]
     half_block = span_tokens // 2
     lat_width = uv_w.shape[1]
+
+    def send_latents(_):
+        latents_across.start()
 
     def gather_latents(_):
         latents_across.wait_recv()
@@ -364,29 +399,32 @@
             load.wait()
 
     def attend(head):
-        scores = dot_f32(keys[...], query_t[head]) * score_scale
-        visible = seen[...] > 0.5
+        pair = range(head, min(head + 2, query_t.shape[0]))
+        wide_query = jnp.concatenate([query_t[at] for at in pair], axis=1)
+        visible = jnp.concatenate([seen[...] for _ in pair], axis=1) > 0.5
+        scores = dot_f32(keys[...], wide_query) * score_scale
         masked = jnp.where(visible, scores, neg_fill)
         top = jnp.max(masked, axis=0, keepdims=True)
         weights = jnp.where(visible, jnp.exp(masked - top), 0.0)
         totals = jnp.sum(weights, axis=0, keepdims=True)
         blended = dot_f32(value_t[...], weights.astype(jnp.bfloat16))
         latent_out = (blended / totals).astype(jnp.bfloat16)
-        attended_ref[head] = dot_first(latent_out, uv_w[head]).astype(jnp.bfloat16)
+        for spot, at in enumerate(pair):
+            span = slice(spot * span_tokens, (spot + 1) * span_tokens)
+            attended_ref[at] = dot_first(latent_out[:, span], uv_w[at]).astype(jnp.bfloat16)
 
     def forward(k):
         for copy in dispatch(k):
             copy.wait_recv()
+        if k == half:
+            for other in near:
+                fan_out(other).start()
+        elif k > half:
+            fan_out(k - half).wait_recv()
         if k not in wide:
             across(k).start()
         for copy in beside(k):
             copy.start()
-
-    def weights(at):
-        piece = at + 1
-        if piece < down_parts:
-            share_down(1, piece).start()
-            share_down(2, piece).start()
 
     def pass_on(k):
         if k not in wide:
@@ -412,6 +450,7 @@
             copy.start()
 
     waiting = [loads[4]]
+    is_full = jnp.max(row_of(place, 0), axis=1, keepdims=True) >= float(base)
 
     def down(k):
         while waiting:
@@ -424,33 +463,54 @@
         total = dot_f32(hidden[k, 0], down_w[0])
         for block in range(1, 4):
             total += dot_f32(hidden[k, block], down_w[block])
-        if k:
+        if k == 0:
+            returned[slots(0)] = total.astype(jnp.bfloat16)
+            return
+        if k >= half:
+            back_send[k, low_rows] = total[:base].astype(jnp.bfloat16)
+            back_send[k, high_rows] = jnp.where(is_full, total[base:], 0.0).astype(jnp.bfloat16)
+        else:
             back_send[k] = total.astype(jnp.bfloat16)
-            give_back(k).start()
-        else:
-            returned[me] = total.astype(jnp.bfloat16)
+        if k > half:
+            collect(k - half).start()
+        give_back(k).start()
+
+    def settle(_):
+        extra = back_send[half, high_rows].astype(jnp.float32)
+        for k in near:
+            collect(k).wait_recv()
+            extra += collected[k].astype(jnp.float32)
+        settled[...] = extra.astype(jnp.bfloat16)
+        settle_extra().start()
 
     stages = {
         "forward": forward, "pass_on": pass_on, "compute": compute, "down": down,
-        "attend": attend, "latents": gather_latents, "weights": weights,
+        "attend": attend, "latents": send_latents, "gather": gather_latents,
+        "settle": settle,
     }
     for stage, at in plan(count, query_t.shape[0]):
         stages[stage](at)
 
+    def share_of(k, first_slot, last_slot):
+        return one_hot(k, first_slot, last_slot) * row_of(gate_of, k)
+
+    extra = share_of(half, base, capacity)
+    for k in far[1:]:
+        extra += share_of(k, base, capacity)
     spread = jnp.concatenate(
-        [
-            jnp.where(place[e : e + 1, :] == slot_at, gate_of[e : e + 1, :], 0.0)
-            for e in range(count)
-        ],
+        [share_of(k, 0, capacity) for k in range(half)]
+        + [share_of(k, 0, base) for k in far]
+        + [extra],
         axis=0,
     )
     high = spread.astype(jnp.bfloat16)
     low = (spread - high.astype(jnp.float32)).astype(jnp.bfloat16)
     for k in range(1, count):
         give_back(k).wait_recv()
-    back = returned[...].reshape(count * capacity, width)
+    settle_extra().wait_recv()
+    back = returned[...]
     out_ref[...] = (dot_first(high, back) + dot_first(low, back)).astype(jnp.bfloat16)
-    for copy in (latents_across, latents_beside, latents_relay):
+    for copy in (latents_across, latents_beside, latents_relay, settle_extra()):
         copy.wait_send()
     for i in range(3):
         for piece in range(down_parts):
@@ -459,10 +519,17 @@
         copies = share_hidden(k)
         if k:
             copies += dispatch(k) + beside(k) + [give_back(k)]
+            if k < half:
+                copies += [fan_out(k), collect(k)]
             if k not in wide:
                 copies += [across(k), relay(k)]
         for copy in copies:
             copy.wait_send()
+
+
+def base_rows(row_count, capacity, count):
+    spare = -(-(row_count - capacity) // (count - 1))
+    return 16 * -(-spare // 16)
 
 
 def window_fused(
@@ -479,14 +546,17 @@
     count = lax.axis_size("exp")
     width = model_width // ways
     capacity = 3 * token_count * picks // (2 * count)
-    wide = tuple(range(1, count // 2))
+    half = count // 2
+    wide = tuple(range(1, half))
+    base = base_rows(token_count * picks, capacity, count)
+    rest = capacity - base
     vmem = pl.BlockSpec(memory_space=pltpu.VMEM)
     hbm = pl.BlockSpec(memory_space=pltpu.HBM)
     block = (capacity, width)
     dtype = jnp.bfloat16
     dma = pltpu.SemaphoreType.DMA
     routed, attended = pl.pallas_call(
-        functools.partial(window_kernel, count, capacity, wide),
+        functools.partial(window_kernel, count, capacity, base, wide),
         out_shape=(
             jax.ShapeDtypeStruct((token_count, width), dtype),
             jax.ShapeDtypeStruct((heads, query_tokens, value_width), dtype),
@@ -509,11 +579,14 @@
             pltpu.VMEM((key_count, query_tokens), jnp.float32),
             pltpu.VMEM((count, token_count), jnp.float32),
             pltpu.VMEM((count, token_count), jnp.float32),
-            pltpu.VMEM((count, 2) + block, dtype),
+            pltpu.VMEM((half, 2) + block, dtype),
+            pltpu.VMEM((half * base + rest, width), dtype),
             pltpu.VMEM((ways, count) + block, dtype),
             pltpu.VMEM((count, ways, capacity, fan), dtype),
             pltpu.VMEM((count,) + block, dtype),
-            pltpu.VMEM((count,) + block, dtype),
+            pltpu.VMEM((half, rest, width), dtype),
+            pltpu.VMEM((rest, width), dtype),
+            pltpu.VMEM((half * (capacity + base) + rest, width), dtype),
             dma((10,)), dma((3,)), dma((3,)),
             dma((count, 2)), dma((count, 2)),
             dma((count,)), dma((count,)),
@@ -522,6 +595,9 @@
             dma((count, 3)), dma((count, 3)),
             dma((3, down_parts)), dma((3, down_parts)),
             dma((count,)), dma((count,)),
+            dma((half,)), dma((half,)),
+            dma((half,)), dma((half,)),
+            dma((1,)), dma((1,)),
         ],
         compiler_params=pltpu.CompilerParams(
             collective_id=0, has_side_effects=True, vmem_limit_bytes=40 * 1024 * 1024
@@ -547,6 +623,8 @@
     capacity = 3 * token_count * picks // (2 * count)
     fits = ways == 4 and count & (count - 1) == 0 and count >= 4 and capacity % 16 == 0
     fits = fits and moe_tokens.shape[1] % (128 * ways) == 0 and block_starts.shape[0] == 8
+    base = base_rows(token_count * picks, capacity, count)
+    fits = fits and base < capacity and count >= 8
     fits = fits and picks == 2 and w_gate.shape[2] % 128 == 0
     if fits:
         return window_fused(

time: 81.8 us -> 70.5 us (0.86)
  Pallas kernels: 79.3 us -> 68 us
    pallas_call x1, Pallas kernels: 79.3 us -> 68 us  [window_fused(): pl.pallas_call(functools.partial(window_kernel, count, capacity, base, wi...]
where the time goes in v2:
time: 70.5 us; the launch traced here: 70.3 us
  Pallas kernels  68 us (96%)
  local copies, waits for them, and re-layouts  1.64 us (2%)
    pallas_call x1, Pallas kernels, window_fused(): pl.pallas_call(functools.partial(window_kernel, count, capacity, base, wi...  68 us
    unnamed x2, local copies, waits for them, and re-layouts  1.64 us

profile of v2, /device:TPU:0, one launch (start us, length us, event | category | flops | bytes accessed | tf_op | source)
XLA Modules:
  0.0 70.3 jit_solution(7839834098410182362)
XLA Ops:
  0.6 68.0 %shard_map.113 = (bf16[128,1792]{1,0:T(8,128)(2,1)S(1)}, bf16[8,128,128]{2,1,0:T(8,128)(2,1)S(1)}) custom-call(s32[2,128]{1,0:T(2,128)} %bitcast.8, f32[2,128]{1,0:T(2,128)} %bitcast.9, bf16[576,128]{1,0:T(8,128)(2,1)} %bitcast.7, bf16[128,7168]{1,0:T(8,128)(2,1)} %tokens_hbm.1, s32[8]{0:T(128)} %starts_hbm.1, bf16[1,7168,128]{2,1,0:T(8,128)(2,1)} %gate_hbm.1, ...), custom_call_target="tpu_custom_call" | custom-call | tf_op jit(solution)/shard_map/pallas_call | solution.py:558
  68.7 0.9 %copy.12 = bf16[128,8,128]{2,1,0:T(8,128)(2,1)} copy(bf16[128,8,128]{2,0,1:T(8,128)(2,1)S(1)} %bitcast.5) | data formatting | bytes 524288
  69.6 0.8 %copy.14 = bf16[128,1792]{1,0:T(8,128)(2,1)} copy(bf16[128,1792]{1,0:T(8,128)(2,1)S(1)} %get-tuple-element.11) | data formatting | bytes 917504

commit v3 on v2

--- a/solution.py
+++ b/solution.py
@@ -116,28 +116,42 @@
     return flipped
 
 
-down_parts = 1
+down_parts = 4
+
+
+def far_order(count):
+    half = count // 2
+    return [half, half + 1] + list(range(count - 1, half + 1, -1))
 
 
 def plan(count, heads):
     half = count // 2
-    near, far = list(range(1, half)), list(range(half, count))
-    order = [("compute", 0)]
-    order += [("forward", k) for k in near[:-1]]
-    order += [("compute", k) for k in near[:-1]]
-    order += [("forward", far[0]), ("forward", near[-1]), ("compute", near[-1])]
-    order += [("down", 0)] + [("down", k) for k in near[:-1]]
-    order += [("forward", far[1]), ("pass_on", far[0]), ("down", near[-1]), ("compute", far[0])]
-    order += [("forward", far[2])]
-    for at in range(1, len(far)):
-        order += [("pass_on", far[at]), ("down", far[at - 1]), ("compute", far[at])]
-        if at + 2 < len(far):
-            order += [("forward", far[at + 2])]
-        elif at + 2 == len(far):
-            order += [("latents", 0)]
-    order += [("gather", 0), ("down", far[-1])]
-    order += [("attend", 0), ("attend", 2), ("settle", 0)]
-    order += [("attend", head) for head in range(4, heads, 2)]
+    near, far = list(range(1, half)), far_order(count)
+    last, late = far[-1], near[2:]
+    order = [("compute", 0), ("forward", far[0])]
+    order += [("send", k) for k in far[2:] + late]
+    order += [("weights", down_parts - 1), ("prepare", 0)]
+    order += [("forward", k) for k in near[:2]] + [("compute", k) for k in near[:2]]
+    order += [("pass_on", far[0]), ("compute", far[0])]
+    order += [("forward", far[1]), ("forward", far[2])]
+    order += [("gated", k) for k in [0] + near[:2]]
+    order += [("down", 0), ("gated", far[0]), ("down", near[0]), ("down", far[0])]
+    order += [("pass_on", far[1]), ("down", near[1]), ("compute", far[1])]
+    for at in range(2, len(far)):
+        k, before = far[at], far[at - 1]
+        if at + 1 < len(far):
+            order += [("forward", far[at + 1])] + [("forward", other) for other in late]
+        order += [("pass_on", k)]
+        if k == last:
+            order += [("gated", other) for other in late + [before]]
+            order += [("compute", k), ("down", before), ("gated", k), ("latents", 0)]
+        else:
+            order += [("compute", other) for other in late]
+            order += [("compute", k), ("gated", before), ("down", before)]
+    order += [("down", last)] + [("down", k) for k in late]
+    order += [("gather", 0)]
+    order += [("attend", head) for head in range(0, heads - 4, 2)]
+    order += [("settle", 0), ("attend", heads - 4), ("attend", heads - 2)]
     return order
 
 
@@ -155,7 +169,7 @@
     count, capacity, base, wide, ids_hbm, gates_hbm, latents_hbm, tokens_hbm, starts_hbm, gate_hbm, up_hbm,
     down_hbm, queries_hbm, uv_hbm, out_ref, attended_ref,
     ids, gates, latents, tokens, starts, pair_w, down_w, query_t, uv_w, every_latent, keys, value_t, seen, place, gate_of,
-    outgoing, far_rows, arrived, hidden, back_send, collected, settled, returned,
+    outgoing, far_rows, arrived, hidden, back_send, collected, settled, returned, share, mixed,
     load_sem, lat_s, lat_r, out_s, out_r, side_s, side_r, near_s, near_r, relay_s, relay_r,
     hid_s, hid_r, wd_s, wd_r, back_s, back_r, fan_s, fan_r, collect_s, collect_r, settle_s, settle_r,
 ):
@@ -191,8 +205,6 @@
         pltpu.make_async_copy(uv_hbm, uv_w, load_sem.at[4]),
         pltpu.make_async_copy(down_hbm.at[0, :, columns(ctx)], down_w.at[ctx], load_sem.at[2]),
     ]
-    for load in loads:
-        load.start()
 
     barrier = pltpu.get_barrier_semaphore()
     for k in range(1, count):
@@ -215,6 +227,7 @@
     half = count // 2
     rest = capacity - base
     far, near = list(range(half, count)), list(range(1, half))
+    sequence = far_order(count)
 
     def far_start(k):
         return (k - half) * base + (rest if k > half else 0)
@@ -225,7 +238,7 @@
     def slots(k):
         if k < half:
             return pl.ds(k * capacity, capacity)
-        return pl.ds(half * capacity + (k - half) * base, base)
+        return pl.ds(half * capacity + sequence.index(k) * base, base)
 
     extra_slots = pl.ds(half * (capacity + base), rest)
     low_rows, high_rows = pl.ds(0, base), pl.ds(base, rest)
@@ -272,8 +285,12 @@
         block = hidden.at[k, ctx]
         return [
             remote(block, block, hid_s.at[k, i], hid_r.at[k, i], me, peer)
-            for i, peer in enumerate(peers)
+            for i, peer in enumerate((other_core, other_row))
         ]
+
+    def relay_hidden(k):
+        block = hidden.at[k, other_row]
+        return remote(block, block, hid_s.at[k, 2], hid_r.at[k, 2], me, other_core)
 
     def share_down(i, piece):
         rows = pl.ds(piece * part, part)
@@ -309,6 +326,10 @@
     latents_across = own_latents(1, other_row)
     latents_relay = remote(row_block, row_block, lat_s.at[2], lat_r.at[2], me, other_core)
 
+    pl.semaphore_wait(barrier, count + 2)
+    for piece in range(down_parts - 1):
+        for i in (1, 2):
+            share_down(i, piece).start()
     inputs[0].wait()
     inputs[3].wait()
     expert_at = lax.broadcasted_iota(jnp.int32, (count, token_count), 0)
@@ -346,23 +367,25 @@
             extra += one_hot(k, base, capacity)
         far_rows[...] = take(jnp.concatenate(picks[:1] + [extra] + picks[1:], axis=0), ctx)
 
+    def send(k):
+        for copy in dispatch(k):
+            copy.start()
+
     inputs[1].wait()
     select(near, 0, ctx)
     if wide:
         select(list(wide), 1, other_row)
+    send(near[1])
+    send(near[0])
+    select_far()
+    send(sequence[0])
+    send(sequence[1])
+    for load in loads:
+        load.start()
+    for piece in range(down_parts):
+        share_down(0, piece).start()
     inputs[2].wait()
-    pl.semaphore_wait(barrier, count + 2)
-    for k in near:
-        for copy in dispatch(k):
-            copy.start()
-    for i in (1, 2, 0):
-        for piece in range(down_parts):
-            share_down(i, piece).start()
     latents_beside.start()
-    select_far()
-    for k in far:
-        for copy in dispatch(k):
-            copy.start()
     every_latent[ctx] = latents[...]
     mine = one_hot(0, 0, capacity).astype(jnp.bfloat16)
     for quarter in range(4):
@@ -417,14 +440,18 @@
         for copy in dispatch(k):
             copy.wait_recv()
         if k == half:
-            for other in near:
-                fan_out(other).start()
+            for other in sequence[1:]:
+                fan_out(other - half).start()
         elif k > half:
             fan_out(k - half).wait_recv()
         if k not in wide:
             across(k).start()
         for copy in beside(k):
             copy.start()
+
+    def weights(piece):
+        for i in (1, 2):
+            share_down(i, piece).start()
 
     def pass_on(k):
         if k not in wide:
@@ -458,8 +485,8 @@
             for i in range(3):
                 for piece in range(down_parts):
                     share_down(i, piece).wait_recv()
-        for copy in share_hidden(k):
-            copy.wait_recv()
+        share_hidden(k)[0].wait_recv()
+        relay_hidden(k).wait_recv()
         total = dot_f32(hidden[k, 0], down_w[0])
         for block in range(1, 4):
             total += dot_f32(hidden[k, block], down_w[block])
@@ -475,6 +502,10 @@
             collect(k - half).start()
         give_back(k).start()
 
+    def gated(k):
+        share_hidden(k)[1].wait_recv()
+        relay_hidden(k).start()
+
     def settle(_):
         extra = back_send[half, high_rows].astype(jnp.float32)
         for k in near:
@@ -483,40 +514,55 @@
         settled[...] = extra.astype(jnp.bfloat16)
         settle_extra().start()
 
+    early = half * capacity + (half - 2) * base
+    total_rows = half * (capacity + base) + rest
+
+    def prepare(_):
+        def share_of(k, first_slot, last_slot):
+            return one_hot(k, first_slot, last_slot) * row_of(gate_of, k)
+
+        extra = share_of(half, base, capacity)
+        for k in far[1:]:
+            extra += share_of(k, base, capacity)
+        spread = jnp.concatenate(
+            [share_of(k, 0, capacity) for k in range(half)]
+            + [share_of(k, 0, base) for k in sequence]
+            + [extra],
+            axis=0,
+        )
+        pad = jnp.zeros((share.shape[2] - total_rows, token_count), jnp.float32)
+        spread = jnp.concatenate([spread, pad], axis=0).T
+        high = spread.astype(jnp.bfloat16)
+        share[0] = high
+        share[1] = (spread - high.astype(jnp.float32)).astype(jnp.bfloat16)
+
+    def mix(first_row, last_row):
+        rows = returned[first_row:last_row]
+        high, low = share[0, :, first_row:last_row], share[1, :, first_row:last_row]
+        return dot_f32(high, rows) + dot_f32(low, rows)
+
     stages = {
         "forward": forward, "pass_on": pass_on, "compute": compute, "down": down,
-        "attend": attend, "latents": send_latents, "gather": gather_latents,
-        "settle": settle,
+        "attend": attend, "latents": send_latents, "gather": gather_latents, "weights": weights,
+        "settle": settle, "prepare": prepare, "send": send, "gated": gated,
     }
     for stage, at in plan(count, query_t.shape[0]):
         stages[stage](at)
 
-    def share_of(k, first_slot, last_slot):
-        return one_hot(k, first_slot, last_slot) * row_of(gate_of, k)
-
-    extra = share_of(half, base, capacity)
-    for k in far[1:]:
-        extra += share_of(k, base, capacity)
-    spread = jnp.concatenate(
-        [share_of(k, 0, capacity) for k in range(half)]
-        + [share_of(k, 0, base) for k in far]
-        + [extra],
-        axis=0,
-    )
-    high = spread.astype(jnp.bfloat16)
-    low = (spread - high.astype(jnp.float32)).astype(jnp.bfloat16)
-    for k in range(1, count):
+    for k in near + sequence[: half - 2]:
+        give_back(k).wait_recv()
+    mixed[...] = mix(0, early)
+    for k in sequence[half - 2 :]:
         give_back(k).wait_recv()
     settle_extra().wait_recv()
-    back = returned[...]
-    out_ref[...] = (dot_first(high, back) + dot_first(low, back)).astype(jnp.bfloat16)
+    out_ref[...] = (mixed[...] + mix(early, total_rows)).astype(jnp.bfloat16)
     for copy in (latents_across, latents_beside, latents_relay, settle_extra()):
         copy.wait_send()
     for i in range(3):
         for piece in range(down_parts):
             share_down(i, piece).wait_send()
     for k in range(count):
-        copies = share_hidden(k)
+        copies = share_hidden(k) + [relay_hidden(k)]
         if k:
             copies += dispatch(k) + beside(k) + [give_back(k)]
             if k < half:
@@ -550,6 +596,7 @@
     wide = tuple(range(1, half))
     base = base_rows(token_count * picks, capacity, count)
     rest = capacity - base
+    share_width = 128 * -(-(half * (capacity + base) + rest) // 128)
     vmem = pl.BlockSpec(memory_space=pltpu.VMEM)
     hbm = pl.BlockSpec(memory_space=pltpu.HBM)
     block = (capacity, width)
@@ -587,6 +634,8 @@
             pltpu.VMEM((half, rest, width), dtype),
             pltpu.VMEM((rest, width), dtype),
             pltpu.VMEM((half * (capacity + base) + rest, width), dtype),
+            pltpu.VMEM((2, token_count, share_width), dtype),
+            pltpu.VMEM((token_count, width), jnp.float32),
             dma((10,)), dma((3,)), dma((3,)),
             dma((count, 2)), dma((count, 2)),
             dma((count,)), dma((count,)),

time: 70.5 us -> 68.2 us (0.967)
  Pallas kernels: 68 us -> 65.7 us
    pallas_call x1, Pallas kernels: 68 us -> 65.7 us  [window_fused(): pl.pallas_call(functools.partial(window_kernel, count, capacity, base, wi...]
where the time goes in v3:
time: 68.2 us; the launch traced here: 68 us
  Pallas kernels  65.7 us (96%)
  local copies, waits for them, and re-layouts  1.64 us (2%)
    pallas_call x1, Pallas kernels, window_fused(): pl.pallas_call(functools.partial(window_kernel, count, capacity, base, wi...  65.7 us
    unnamed x2, local copies, waits for them, and re-layouts  1.64 us

profile of v3, /device:TPU:0, one launch (start us, length us, event | category | flops | bytes accessed | tf_op | source)
XLA Modules:
  0.0 68.0 jit_solution(3264667947635469997)
XLA Ops:
  0.6 65.7 %shard_map.113 = (bf16[128,1792]{1,0:T(8,128)(2,1)S(1)}, bf16[8,128,128]{2,1,0:T(8,128)(2,1)S(1)}) custom-call(s32[2,128]{1,0:T(2,128)} %bitcast.8, f32[2,128]{1,0:T(2,128)} %bitcast.9, bf16[576,128]{1,0:T(8,128)(2,1)} %bitcast.7, bf16[128,7168]{1,0:T(8,128)(2,1)} %tokens_hbm.1, s32[8]{0:T(128)} %starts_hbm.1, bf16[1,7168,128]{2,1,0:T(8,128)(2,1)} %gate_hbm.1, ...), custom_call_target="tpu_custom_call" | custom-call | tf_op jit(solution)/shard_map/pallas_call | solution.py:605
  66.4 0.9 %copy.12 = bf16[128,8,128]{2,1,0:T(8,128)(2,1)} copy(bf16[128,8,128]{2,0,1:T(8,128)(2,1)S(1)} %bitcast.5) | data formatting | bytes 524288
  67.2 0.8 %copy.14 = bf16[128,1792]{1,0:T(8,128)(2,1)} copy(bf16[128,1792]{1,0:T(8,128)(2,1)S(1)} %get-tuple-element.11) | data formatting | bytes 917504

commit v4 on v3

--- a/solution.py
+++ b/solution.py
@@ -128,30 +128,23 @@
     half = count // 2
     near, far = list(range(1, half)), far_order(count)
     last, late = far[-1], near[2:]
-    order = [("compute", 0), ("forward", far[0])]
+    order = [("compute", 0), ("forward", far[0]), ("weights", 2), ("weights", 3)]
     order += [("send", k) for k in far[2:] + late]
-    order += [("weights", down_parts - 1), ("prepare", 0)]
-    order += [("forward", k) for k in near[:2]] + [("compute", k) for k in near[:2]]
-    order += [("pass_on", far[0]), ("compute", far[0])]
-    order += [("forward", far[1]), ("forward", far[2])]
-    order += [("gated", k) for k in [0] + near[:2]]
-    order += [("down", 0), ("gated", far[0]), ("down", near[0]), ("down", far[0])]
-    order += [("pass_on", far[1]), ("down", near[1]), ("compute", far[1])]
-    for at in range(2, len(far)):
-        k, before = far[at], far[at - 1]
-        if at + 1 < len(far):
-            order += [("forward", far[at + 1])] + [("forward", other) for other in late]
-        order += [("pass_on", k)]
-        if k == last:
-            order += [("gated", other) for other in late + [before]]
-            order += [("compute", k), ("down", before), ("gated", k), ("latents", 0)]
-        else:
-            order += [("compute", other) for other in late]
-            order += [("compute", k), ("gated", before), ("down", before)]
-    order += [("down", last)] + [("down", k) for k in late]
-    order += [("gather", 0)]
-    order += [("attend", head) for head in range(0, heads - 4, 2)]
-    order += [("settle", 0), ("attend", heads - 4), ("attend", heads - 2)]
+    order += [("prepare", 0), ("forward", near[0]), ("pass_on", far[0])]
+    order += [("compute", near[0]), ("compute", far[0])]
+    order += [("forward", far[1]), ("forward", near[1]), ("forward", far[2]), ("compute", near[1])]
+    order += [("gated", 0), ("gated", far[0]), ("down", 0), ("gated", near[0])]
+    order += [("down", far[0]), ("pass_on", far[1]), ("down", near[0])]
+    order += [("compute", far[1]), ("forward", last), ("gated", near[1])]
+    order += [("pass_on", far[2]), ("down", near[1]), ("gated", far[1]), ("compute", far[2])]
+    order += [("down", far[1])] + [("forward", k) for k in late] + [("pass_on", last)]
+    order += [("compute", last), ("latents", 0), ("gated", far[2]), ("down", far[2])]
+    order += [("gated", last)] + [("pass_on", k) for k in late] + [("down", last), ("give", last)]
+    order += [("compute", k) for k in late] + [("relay", 0)]
+    order += [("gated", k) for k in late]
+    order += [("gather", 0)] + [("down", k) for k in late]
+    order += [("attend", 0), ("settle", 0)]
+    order += [("attend", head) for head in range(2, heads, 2)]
     return order
 
 
@@ -166,10 +159,10 @@
 
 
 def window_kernel(
-    count, capacity, base, wide, ids_hbm, gates_hbm, latents_hbm, tokens_hbm, starts_hbm, gate_hbm, up_hbm,
+    count, capacity, base, ids_hbm, gates_hbm, latents_hbm, tokens_hbm, starts_hbm, gate_hbm, up_hbm,
     down_hbm, queries_hbm, uv_hbm, out_ref, attended_ref,
     ids, gates, latents, tokens, starts, pair_w, down_w, query_t, uv_w, every_latent, keys, value_t, seen, place, gate_of,
-    outgoing, far_rows, arrived, hidden, back_send, collected, settled, returned, share, mixed,
+    outgoing, far_rows, extra_rows, arrived, hidden, back_send, collected, settled, returned, share, mixed,
     load_sem, lat_s, lat_r, out_s, out_r, side_s, side_r, near_s, near_r, relay_s, relay_r,
     hid_s, hid_r, wd_s, wd_r, back_s, back_r, fan_s, fan_r, collect_s, collect_r, settle_s, settle_r,
 ):
@@ -243,42 +236,59 @@
     extra_slots = pl.ds(half * (capacity + base), rest)
     low_rows, high_rows = pl.ds(0, base), pl.ds(base, rest)
 
-    def quarters(k):
-        return (ctx, other_row) if k in wide else (ctx,)
+    wide = near[:2]
+
+    def copies_of(k):
+        return 2 if k in wide else 1
 
     def dispatch(k):
         to = flip_bits(me, k)
+        if k < half:
+            pieces = [
+                (outgoing.at[k, i], arrived.at[quarter, me])
+                for i, quarter in enumerate((ctx, other_row)[: copies_of(k)])
+            ]
+        else:
+            rows = rows_of(k)
+            pieces = [
+                (far_rows.at[pl.ds(far_start(k), rows)], arrived.at[ctx, me, pl.ds(0, rows)])
+            ]
+            if k == half:
+                pieces += [(extra_rows, arrived.at[other_row, me, high_rows])]
+        return [
+            remote(source, target, out_s.at[k, i], out_r.at[k, i], to, ctx)
+            for i, (source, target) in enumerate(pieces)
+        ]
+
+    def fan_out(k):
+        blocks = [arrived.at[row, flip_bits(me, half), high_rows] for row in (ctx, other_row)]
+        return [
+            remote(block, block, fan_s.at[k, i], fan_r.at[k, i], flip_bits(me, k), ctx)
+            for i, block in enumerate(blocks)
+        ]
+
+    def crossing(k, quarter):
+        block = arrived.at[quarter, flip_bits(me, k)]
+        return arrived.at[quarter, flip_bits(me, k), low_rows] if k >= half else block
+
+    def across(k):
+        block = crossing(k, ctx)
+        return remote(block, block, side_s.at[k], side_r.at[k], me, other_row)
+
+    def beside(k):
+        at = flip_bits(me, k)
+        blocks = [arrived.at[ctx, at]]
         if k >= half:
-            rows = rows_of(k)
-            source = far_rows.at[pl.ds(far_start(k), rows)]
-            target = arrived.at[ctx, me, pl.ds(0, rows)]
-            return [remote(source, target, out_s.at[k, 0], out_r.at[k, 0], to, ctx)]
+            blocks += [arrived.at[other_row, at, high_rows]]
+        elif k in wide:
+            blocks += [arrived.at[other_row, at]]
         return [
-            remote(
-                outgoing.at[k, i], arrived.at[quarter, me], out_s.at[k, i], out_r.at[k, i], to, ctx
-            )
-            for i, quarter in enumerate(quarters(k))
+            remote(block, block, near_s.at[k, i], near_r.at[k, i], me, other_core)
+            for i, block in enumerate(blocks)
         ]
 
-    def fan_out(k):
-        block = arrived.at[ctx, flip_bits(me, half), high_rows]
-        return remote(block, block, fan_s.at[k], fan_r.at[k], flip_bits(me, k), ctx)
-
-    def across(k):
-        block = arrived.at[ctx, flip_bits(me, k)]
-        return remote(block, block, side_s.at[k], side_r.at[k], me, other_row)
-
-    def beside(k):
-        return [
-            remote(
-                arrived.at[quarter, flip_bits(me, k)], arrived.at[quarter, flip_bits(me, k)],
-                near_s.at[k, i], near_r.at[k, i], me, other_core,
-            )
-            for i, quarter in enumerate(quarters(k))
-        ]
-
     def relay(k):
-        block = arrived.at[other_row, flip_bits(me, k)]
+        block = crossing(k, other_row)
         return remote(block, block, relay_s.at[k], relay_r.at[k], me, other_core)
 
     def share_hidden(k):
@@ -327,7 +337,7 @@
     latents_relay = remote(row_block, row_block, lat_s.at[2], lat_r.at[2], me, other_core)
 
     pl.semaphore_wait(barrier, count + 2)
-    for piece in range(down_parts - 1):
+    for piece in range(2):
         for i in (1, 2):
             share_down(i, piece).start()
     inputs[0].wait()
@@ -366,19 +376,19 @@
         for k in far[1:]:
             extra += one_hot(k, base, capacity)
         far_rows[...] = take(jnp.concatenate(picks[:1] + [extra] + picks[1:], axis=0), ctx)
+        extra_rows[...] = take(extra, other_row)
 
     def send(k):
         for copy in dispatch(k):
             copy.start()
 
     inputs[1].wait()
+    select_far()
+    send(sequence[0])
     select(near, 0, ctx)
-    if wide:
-        select(list(wide), 1, other_row)
+    select(wide, 1, other_row)
     send(near[1])
     send(near[0])
-    select_far()
-    send(sequence[0])
     send(sequence[1])
     for load in loads:
         load.start()
@@ -399,9 +409,11 @@
     def send_latents(_):
         latents_across.start()
 
-    def gather_latents(_):
+    def relay_latents(_):
         latents_across.wait_recv()
         latents_relay.start()
+
+    def gather_latents(_):
         inputs[4].wait()
         key_at = lax.broadcasted_iota(jnp.int32, (4 * span_tokens, span_tokens), 0)
         own_at = lax.broadcasted_iota(jnp.int32, (4 * span_tokens, span_tokens), 1)
@@ -441,9 +453,11 @@
             copy.wait_recv()
         if k == half:
             for other in sequence[1:]:
-                fan_out(other - half).start()
+                for copy in fan_out(other - half):
+                    copy.start()
         elif k > half:
-            fan_out(k - half).wait_recv()
+            for copy in fan_out(k - half):
+                copy.wait_recv()
         if k not in wide:
             across(k).start()
         for copy in beside(k):
@@ -454,9 +468,8 @@
             share_down(i, piece).start()
 
     def pass_on(k):
-        if k not in wide:
-            across(k).wait_recv()
-            relay(k).start()
+        across(k).wait_recv()
+        relay(k).start()
 
     def compute(k):
         if k:
@@ -500,6 +513,10 @@
             back_send[k] = total.astype(jnp.bfloat16)
         if k > half:
             collect(k - half).start()
+        if k != sequence[-1]:
+            give_back(k).start()
+
+    def give(k):
         give_back(k).start()
 
     def gated(k):
@@ -543,7 +560,7 @@
 
     stages = {
         "forward": forward, "pass_on": pass_on, "compute": compute, "down": down,
-        "attend": attend, "latents": send_latents, "gather": gather_latents, "weights": weights,
+        "attend": attend, "latents": send_latents, "gather": gather_latents, "relay": relay_latents, "give": give, "weights": weights,
         "settle": settle, "prepare": prepare, "send": send, "gated": gated,
     }
     for stage, at in plan(count, query_t.shape[0]):
@@ -566,7 +583,7 @@
         if k:
             copies += dispatch(k) + beside(k) + [give_back(k)]
             if k < half:
-                copies += [fan_out(k), collect(k)]
+                copies += fan_out(k) + [collect(k)]
             if k not in wide:
                 copies += [across(k), relay(k)]
         for copy in copies:
@@ -593,7 +610,6 @@
     width = model_width // ways
     capacity = 3 * token_count * picks // (2 * count)
     half = count // 2
-    wide = tuple(range(1, half))
     base = base_rows(token_count * picks, capacity, count)
     rest = capacity - base
     share_width = 128 * -(-(half * (capacity + base) + rest) // 128)
@@ -603,7 +619,7 @@
     dtype = jnp.bfloat16
     dma = pltpu.SemaphoreType.DMA
     routed, attended = pl.pallas_call(
-        functools.partial(window_kernel, count, capacity, base, wide),
+        functools.partial(window_kernel, count, capacity, base),
         out_shape=(
             jax.ShapeDtypeStruct((token_count, width), dtype),
             jax.ShapeDtypeStruct((heads, query_tokens, value_width), dtype),
@@ -628,6 +644,7 @@
             pltpu.VMEM((count, token_count), jnp.float32),
             pltpu.VMEM((half, 2) + block, dtype),
             pltpu.VMEM((half * base + rest, width), dtype),
+            pltpu.VMEM((rest, width), dtype),
             pltpu.VMEM((ways, count) + block, dtype),
             pltpu.VMEM((count, ways, capacity, fan), dtype),
             pltpu.VMEM((count,) + block, dtype),
@@ -644,7 +661,7 @@
             dma((count, 3)), dma((count, 3)),
             dma((3, down_parts)), dma((3, down_parts)),
             dma((count,)), dma((count,)),
-            dma((half,)), dma((half,)),
+            dma((half, 2)), dma((half, 2)),
             dma((half,)), dma((half,)),
             dma((1,)), dma((1,)),
         ],

time: 68.2 us -> 67.2 us (0.985)
  Pallas kernels: 65.7 us -> 64.8 us
    pallas_call x1, Pallas kernels: 65.7 us -> 64.8 us  [window_fused(): pl.pallas_call(functools.partial(window_kernel, count, capacity, base), o...]
where the time goes in v4:
time: 67.2 us; the launch traced here: 67.1 us
  Pallas kernels  64.8 us (96%)
  local copies, waits for them, and re-layouts  1.64 us (2%)
    pallas_call x1, Pallas kernels, window_fused(): pl.pallas_call(functools.partial(window_kernel, count, capacity, base), o...  64.8 us
    unnamed x2, local copies, waits for them, and re-layouts  1.64 us

profile of v4, /device:TPU:0, one launch (start us, length us, event | category | flops | bytes accessed | tf_op | source)
XLA Modules:
  0.0 67.1 jit_solution(4668425964662481969)
XLA Ops:
  0.6 64.8 %shard_map.113 = (bf16[128,1792]{1,0:T(8,128)(2,1)S(1)}, bf16[8,128,128]{2,1,0:T(8,128)(2,1)S(1)}) custom-call(s32[2,128]{1,0:T(2,128)} %bitcast.8, f32[2,128]{1,0:T(2,128)} %bitcast.9, bf16[576,128]{1,0:T(8,128)(2,1)} %bitcast.7, bf16[128,7168]{1,0:T(8,128)(2,1)} %tokens_hbm.1, s32[8]{0:T(128)} %starts_hbm.1, bf16[1,7168,128]{2,1,0:T(8,128)(2,1)} %gate_hbm.1, ...), custom_call_target="tpu_custom_call" | custom-call | tf_op jit(solution)/shard_map/pallas_call | solution.py:621
  65.4 0.9 %copy.12 = bf16[128,8,128]{2,1,0:T(8,128)(2,1)} copy(bf16[128,8,128]{2,0,1:T(8,128)(2,1)S(1)} %bitcast.5) | data formatting | bytes 524288
  66.3 0.8 %copy.14 = bf16[128,1792]{1,0:T(8,128)(2,1)} copy(bf16[128,1792]{1,0:T(8,128)(2,1)S(1)} %get-tuple-element.11) | data formatting | bytes 917504

commit v5 on v4

--- a/solution.py
+++ b/solution.py
@@ -163,8 +163,8 @@
     down_hbm, queries_hbm, uv_hbm, out_ref, attended_ref,
     ids, gates, latents, tokens, starts, pair_w, down_w, query_t, uv_w, every_latent, keys, value_t, seen, place, gate_of,
     outgoing, far_rows, extra_rows, arrived, hidden, back_send, collected, settled, returned, share, mixed,
-    load_sem, lat_s, lat_r, out_s, out_r, side_s, side_r, near_s, near_r, relay_s, relay_r,
-    hid_s, hid_r, wd_s, wd_r, back_s, back_r, fan_s, fan_r, collect_s, collect_r, settle_s, settle_r,
+    load_sem, lat_s, lat_r, sent, out_r, side_r, near_r, relay_r,
+    hid_r, wd_r, back_r, fan_r, collect_r, settle_r,
 ):
     me = lax.axis_index("exp")
     ctx = lax.axis_index("ctx")
@@ -256,14 +256,14 @@
             if k == half:
                 pieces += [(extra_rows, arrived.at[other_row, me, high_rows])]
         return [
-            remote(source, target, out_s.at[k, i], out_r.at[k, i], to, ctx)
+            remote(source, target, sent.at[0], out_r.at[k, i], to, ctx)
             for i, (source, target) in enumerate(pieces)
         ]
 
     def fan_out(k):
         blocks = [arrived.at[row, flip_bits(me, half), high_rows] for row in (ctx, other_row)]
         return [
-            remote(block, block, fan_s.at[k, i], fan_r.at[k, i], flip_bits(me, k), ctx)
+            remote(block, block, sent.at[0], fan_r.at[k, i], flip_bits(me, k), ctx)
             for i, block in enumerate(blocks)
         ]
 
@@ -273,7 +273,7 @@
 
     def across(k):
         block = crossing(k, ctx)
-        return remote(block, block, side_s.at[k], side_r.at[k], me, other_row)
+        return remote(block, block, sent.at[0], side_r.at[k], me, other_row)
 
     def beside(k):
         at = flip_bits(me, k)
@@ -283,46 +283,46 @@
         elif k in wide:
             blocks += [arrived.at[other_row, at]]
         return [
-            remote(block, block, near_s.at[k, i], near_r.at[k, i], me, other_core)
+            remote(block, block, sent.at[0], near_r.at[k, i], me, other_core)
             for i, block in enumerate(blocks)
         ]
 
     def relay(k):
         block = crossing(k, other_row)
-        return remote(block, block, relay_s.at[k], relay_r.at[k], me, other_core)
+        return remote(block, block, sent.at[0], relay_r.at[k], me, other_core)
 
     def share_hidden(k):
         block = hidden.at[k, ctx]
         return [
-            remote(block, block, hid_s.at[k, i], hid_r.at[k, i], me, peer)
+            remote(block, block, sent.at[2], hid_r.at[k, i], me, peer)
             for i, peer in enumerate((other_core, other_row))
         ]
 
     def relay_hidden(k):
         block = hidden.at[k, other_row]
-        return remote(block, block, hid_s.at[k, 2], hid_r.at[k, 2], me, other_core)
+        return remote(block, block, sent.at[2], hid_r.at[k, 2], me, other_core)
 
     def share_down(i, piece):
         rows = pl.ds(piece * part, part)
         return remote(
             down_hbm.at[0, rows, columns(peers[i])], down_w.at[ctx, rows],
-            wd_s.at[i, piece], wd_r.at[i, piece], me, peers[i],
+            sent.at[3], wd_r.at[0], me, peers[i],
         )
 
     def give_back(k):
         to = flip_bits(me, k)
         source = back_send.at[k, low_rows] if k >= half else back_send.at[k]
-        return remote(source, returned.at[slots(k)], back_s.at[k], back_r.at[k], to, ctx)
+        return remote(source, returned.at[slots(k)], sent.at[0 if k >= half else 1], back_r.at[k], to, ctx)
 
     def collect(k):
         return remote(
-            back_send.at[k + half, high_rows], collected.at[k], collect_s.at[k], collect_r.at[k],
+            back_send.at[k + half, high_rows], collected.at[k], sent.at[0], collect_r.at[k],
             flip_bits(me, k), ctx,
         )
 
     def settle_extra():
         return remote(
-            settled, returned.at[extra_slots], settle_s.at[0], settle_r.at[0],
+            settled, returned.at[extra_slots], sent.at[0], settle_r.at[0],
             flip_bits(me, half), ctx,
         )
 
@@ -490,14 +490,14 @@
             copy.start()
 
     waiting = [loads[4]]
+    three = down_w.at[pl.ds(0, 3)]
+    all_down = remote(three, three, sent.at[3], wd_r.at[0], me, other_core)
     is_full = jnp.max(row_of(place, 0), axis=1, keepdims=True) >= float(base)
 
     def down(k):
         while waiting:
             waiting.pop().wait()
-            for i in range(3):
-                for piece in range(down_parts):
-                    share_down(i, piece).wait_recv()
+            all_down.wait_recv()
         share_hidden(k)[0].wait_recv()
         relay_hidden(k).wait_recv()
         total = dot_f32(hidden[k, 0], down_w[0])
@@ -573,21 +573,12 @@
         give_back(k).wait_recv()
     settle_extra().wait_recv()
     out_ref[...] = (mixed[...] + mix(early, total_rows)).astype(jnp.bfloat16)
-    for copy in (latents_across, latents_beside, latents_relay, settle_extra()):
+    for copy in (latents_across, latents_beside, latents_relay):
         copy.wait_send()
-    for i in range(3):
-        for piece in range(down_parts):
-            share_down(i, piece).wait_send()
-    for k in range(count):
-        copies = share_hidden(k) + [relay_hidden(k)]
-        if k:
-            copies += dispatch(k) + beside(k) + [give_back(k)]
-            if k < half:
-                copies += fan_out(k) + [collect(k)]
-            if k not in wide:
-                copies += [across(k), relay(k)]
-        for copy in copies:
-            copy.wait_send()
+    near_back = back_send.at[pl.ds(0, half - 1)]
+    shares = hidden.at[pl.ds(0, 3 * count // 4)]
+    for ref, spot in ((arrived, 0), (near_back, 1), (shares, 2), (three, 3)):
+        remote(ref, ref, sent.at[spot], wd_r.at[0], me, other_core).wait_send()
 
 
 def base_rows(row_count, capacity, count):
@@ -653,17 +644,9 @@
             pltpu.VMEM((half * (capacity + base) + rest, width), dtype),
             pltpu.VMEM((2, token_count, share_width), dtype),
             pltpu.VMEM((token_count, width), jnp.float32),
-            dma((10,)), dma((3,)), dma((3,)),
-            dma((count, 2)), dma((count, 2)),
-            dma((count,)), dma((count,)),
-            dma((count, 2)), dma((count, 2)),
-            dma((count,)), dma((count,)),
-            dma((count, 3)), dma((count, 3)),
-            dma((3, down_parts)), dma((3, down_parts)),
-            dma((count,)), dma((count,)),
-            dma((half, 2)), dma((half, 2)),
-            dma((half,)), dma((half,)),
-            dma((1,)), dma((1,)),
+            dma((10,)), dma((3,)), dma((3,)), dma((4,)),
+            dma((count, 2)), dma((count,)), dma((count, 2)), dma((count,)),
+            dma((count, 3)), dma((1,)), dma((count,)), dma((half, 2)), dma((half,)), dma((1,)),
         ],
         compiler_params=pltpu.CompilerParams(
             collective_id=0, has_side_effects=True, vmem_limit_bytes=40 * 1024 * 1024
@@ -690,7 +673,7 @@
     fits = ways == 4 and count & (count - 1) == 0 and count >= 4 and capacity % 16 == 0
     fits = fits and moe_tokens.shape[1] % (128 * ways) == 0 and block_starts.shape[0] == 8
     base = base_rows(token_count * picks, capacity, count)
-    fits = fits and base < capacity and count >= 8
+    fits = fits and 3 * base == 2 * capacity and count == 8
     fits = fits and picks == 2 and w_gate.shape[2] % 128 == 0
     if fits:
         return window_fused(

time: 67.2 us -> 66.1 us (0.984)
  Pallas kernels: 64.8 us -> 63.6 us
    pallas_call x1, Pallas kernels: 64.8 us -> 63.6 us  [window_fused(): pl.pallas_call(functools.partial(window_kernel, count, capacity, base), o...]
where the time goes in v5:
time: 66.1 us; the launch traced here: 65.9 us
  Pallas kernels  63.6 us (96%)
  local copies, waits for them, and re-layouts  1.64 us (2%)
    pallas_call x1, Pallas kernels, window_fused(): pl.pallas_call(functools.partial(window_kernel, count, capacity, base), o...  63.6 us
    unnamed x2, local copies, waits for them, and re-layouts  1.64 us

profile of v5, /device:TPU:0, one launch (start us, length us, event | category | flops | bytes accessed | tf_op | source)
XLA Modules:
  0.0 65.9 jit_solution(9578479232217180068)
XLA Ops:
  0.6 63.6 %shard_map.113 = (bf16[128,1792]{1,0:T(8,128)(2,1)S(1)}, bf16[8,128,128]{2,1,0:T(8,128)(2,1)S(1)}) custom-call(s32[2,128]{1,0:T(2,128)} %bitcast.8, f32[2,128]{1,0:T(2,128)} %bitcast.9, bf16[576,128]{1,0:T(8,128)(2,1)} %bitcast.7, bf16[128,7168]{1,0:T(8,128)(2,1)} %tokens_hbm.1, s32[8]{0:T(128)} %starts_hbm.1, bf16[1,7168,128]{2,1,0:T(8,128)(2,1)} %gate_hbm.1, ...), custom_call_target="tpu_custom_call" | custom-call | tf_op jit(solution)/shard_map/pallas_call | solution.py:612
  64.3 0.9 %copy.12 = bf16[128,8,128]{2,1,0:T(8,128)(2,1)} copy(bf16[128,8,128]{2,0,1:T(8,128)(2,1)S(1)} %bitcast.5) | data formatting | bytes 524288
  65.2 0.8 %copy.14 = bf16[128,1792]{1,0:T(8,128)(2,1)} copy(bf16[128,1792]{1,0:T(8,128)(2,1)S(1)} %get-tuple-element.11) | data formatting | bytes 917504
